TPU v7x, 32 devices: a whole 2x2x4 slice. The times are simulated.
32 devices in a mesh: col: 8 (over z, y), row: 4 (over x, core).
Axes of the slice: x: 2, y: 2, z: 4, core: 2. Of those that a mesh axis runs over, the one named last changes fastest.
Arguments:
- vel_x: float32 [36, 2, 96, 2048], P(None, None, 'row', 'col')
- vel_y: float32 [36, 2, 96, 2048], P(None, None, 'row', 'col')
- pot_temp: float32 [36, 2, 96, 2048], P(None, None, 'row', 'col')
- salinity: float32 [36, 2, 96, 2048], P(None, None, 'row', 'col')
- surf_eta: float32 [2, 96, 2048], P(None, 'row', 'col')
- trans_x: float32 [2, 96, 2048], P(None, 'row', 'col')
- trans_y: float32 [2, 96, 2048], P(None, 'row', 'col')
- col_depth: float32 [96, 2048], P('row', 'col')
- wet_levels: int32 [96, 2048], P('row', 'col')
- avg_weights: float32 [30], replicated
Outputs:
- output 1: float32 [2, 96, 2048], P(None, 'row', 'col')
- output 2: float32 [2, 96, 2048], P(None, 'row', 'col')
- output 3: float32 [2, 96, 2048], P(None, 'row', 'col')
- output 4: float32 [36, 2, 96, 2048], P(None, None, 'row', 'col')
- output 5: float32 [36, 2, 96, 2048], P(None, None, 'row', 'col')
- output 6: float32 [36, 2, 96, 2048], P(None, None, 'row', 'col')
- output 7: float32 [36, 2, 96, 2048], P(None, None, 'row', 'col')
All inputs are finite; a program needn't handle non-finite values.
Results may differ from a plain program's by a relative error of at most 0.001.
Values sent between devices are 32-bit elements.
A program may use at most 1 GiB of HBM per device.

v0:
```python
import functools

import jax
import jax.numpy as jnp
from jax import lax
from jax.experimental import pallas as pl
from jax.experimental.pallas import tpu as pltpu
from jax.sharding import PartitionSpec as P

WAVE_COURANT = 0.4
THERM_EXP = 0.2
HALINE_CON = 0.15
PRESS_SCALE = 0.5
VISC_NUMBER = 1.0
DIFF_NUMBER = 0.5

MESH = pl.DeviceIdType.MESH
F32 = jnp.float32
ROWS = 24
PAD = 8
XR = ROWS + 2 * PAD
LEVEL_BLOCK = 4
LANES = 128
TILE = (8, LANES)
RING = 3
M = 2
FRAME = 4 * ROWS + 2 * PAD
HALO = 32


def sweep_constants(level_count, strength):
    inverse, ratio = [], []
    for k in range(level_count):
        pivot = 1.0 + strength if k == 0 else 1.0 + 2.0 * strength - strength * ratio[-1]
        inverse.append(1.0 / pivot)
        ratio.append(strength / pivot)
    return inverse, ratio


def iota(shape, axis):
    return lax.broadcasted_iota(jnp.int32, shape, axis)


def lanes(*lead):
    return iota((*lead, 8, 128), len(lead) + 1)


def turn(x, shift):
    return pltpu.roll(x, shift, x.ndim - 1)


def east(x, keep=3):
    rolled = turn(x, 127)
    following = rolled[1:] if keep == 2 else jnp.concatenate([rolled[1:], rolled[:1]], axis=0)
    return jnp.where(lanes(keep) == 127, following, rolled[:keep])


def west(x, keep=3):
    rolled = turn(x, 1)
    return jnp.where(lanes(keep) == 0, jnp.concatenate([rolled[2:], rolled[:keep - 1]], axis=0), rolled[:keep])


def step_kernel(
    col_count, level_count, sub_count,
    u_hbm, v_hbm, t_hbm, s_hbm, eta_in, tx_in, ty_in, depth_in, wet_in, weights, table,
    xu_hbm, xv_hbm, ct_hbm, cs_hbm, qu_out, qv_out, nuv_out, eta_out, tx_out, ty_out,
    cube, sol,
    col_w, col_e, rcv_e, rcv_w, row_s, row_n, rcv_n, rcv_s, rcv_se, rcv_nw,
    kmt, nuv, sums, stage, stage_w, stage_e, pk_e, pk_w, fstage, fstage_w, fstage_e, fpk_e, fpk_w,
    frame, coef, acc, result, result_in,
    load_sem, store_sem, send_sem, edge_sem, row_sem, e_sem, w_sem, frow_sem, fe_sem, fw_sem, swap_sem,
):
    L = level_count
    U, V, T, S = range(4)
    ETA, TX, TY, DEPTH, FX, FY = range(6)
    OWN = slice(0, 2)
    col = lax.axis_index("col")
    row = lax.axis_index("row")
    chip = row // 2
    core = row % 2
    east_col = lax.rem(col + 1, col_count)
    west_col = lax.rem(col + col_count - 1, col_count)
    peers = [lax.rem(row + d, 4) for d in (1, 2, 3)]
    lane = lanes()
    zero = jnp.zeros(TILE, F32)

    def aligned(start, size=8):
        return pl.ds(pl.multiple_of(start, 8), size)

    barrier = pltpu.get_barrier_semaphore()
    for r in peers:
        pl.semaphore_signal(barrier, inc=1, device_id={"row": r, "col": col}, device_id_type=MESH)
    for other in (east_col, west_col):
        for r in range(4):
            pl.semaphore_signal(barrier, inc=1, device_id={"row": r, "col": other}, device_id_type=MESH)

    loads = []
    for f, src in enumerate((u_hbm, v_hbm, t_hbm, s_hbm)):
        for lt in range(2):
            loads.append(pltpu.make_async_copy(
                src.at[:, :, :, pl.ds(LANES * lt, LANES)], cube.at[f, :, :, lt, pl.ds(PAD, ROWS), :], load_sem.at[2 * f + lt]))
            loads[-1].start()

    def pack_2d(get, count, out_w, out_e):
        for i in range(3):
            rs = pl.ds(8 * i, 8)
            for m in range(2):
                pack_w = pack_e = zero
                for j in range(count):
                    here = lane // HALO == j
                    pack_w = jnp.where(here, turn(get[m, j, 0, rs, :], HALO * j), pack_w)
                    pack_e = jnp.where(here, turn(get[m, j, 1, rs, :], (HALO * j + HALO) % 128), pack_e)
                out_w[m, rs, :] = pack_w
                out_e[m, rs, :] = pack_e

    for lt in range(2):
        ls = pl.ds(LANES * lt, LANES)
        wet = wet_in[:, ls].astype(F32)
        kmt[lt, pl.ds(0, ROWS), :] = wet
        masked = jnp.where(wet > 0.0, depth_in[:, ls], 0.0)
        for m in range(2):
            stage[m, ETA, lt] = eta_in[m, :, ls]
            stage[m, TX, lt] = tx_in[m, :, ls]
            stage[m, TY, lt] = ty_in[m, :, ls]
            stage[m, DEPTH, lt] = masked
    pack_2d(stage, 4, stage_w, stage_e)

    has_s, has_n = row > 0, row < 3

    @pl.when(row == 0)
    def _():
        rcv_s[...] = jnp.zeros(rcv_s.shape, F32)
        rcv_se[...] = jnp.zeros(rcv_se.shape, F32)

    @pl.when(row == 3)
    def _():
        rcv_n[...] = jnp.zeros(rcv_n.shape, F32)
        rcv_nw[...] = jnp.zeros(rcv_nw.shape, F32)

    frame[:, :, pl.ds(0, PAD), :] = jnp.zeros((6, 3, PAD, 128), F32)
    frame[:, :, pl.ds(PAD + 4 * ROWS, PAD), :] = jnp.zeros((6, 3, PAD, 128), F32)

    for copy in loads:
        copy.wait()

    lane42 = lanes(4, 2)

    def pack(k, carry):
        west_pack, east_pack = carry
        for i in range(3):
            slot = L * i + k
            rs = pl.ds(PAD + 8 * i, 8)
            west_pack = jnp.where(lane42 == slot, turn(cube[:, k, :, 0, rs, :], slot), west_pack)
            east_pack = jnp.where(lane42 == slot, turn(cube[:, k, :, 1, rs, :], slot + 1), east_pack)
        return west_pack, east_pack

    empty = jnp.zeros((4, 2, 8, 128), F32)
    west_pack, east_pack = lax.fori_loop(0, L, pack, (empty, empty))
    col_w[...] = west_pack
    col_e[...] = east_pack
    for i in range(3):
        slot = 3 * L + i
        col_w[0, 0] = jnp.where(lane == slot, turn(kmt[0, pl.ds(8 * i, 8), :], slot), col_w[0, 0])

    sub42 = iota((4, 2, 8, 128), 2)

    def pack_rows(g, carry):
        low = high = empty
        for j in range(8):
            k, m = 4 * g + j // 2, j % 2
            low = jnp.where(sub42 == j, cube[:, k, m, OWN, pl.ds(PAD - j, 8), :], low)
            high = jnp.where(sub42 == j, cube[:, k, m, OWN, pl.ds(PAD + ROWS - 1 - j, 8), :], high)
        row_s[:, :, aligned(8 * g), :] = low
        row_n[:, :, aligned(8 * g), :] = high
        return carry

    lax.fori_loop(0, L // 4, pack_rows, 0)
    for f in range(4):
        row_s[f, :, pl.ds(2 * L, 8), :] = kmt[:, pl.ds(0, 8), :]
        row_n[f, :, pl.ds(2 * L, 8), :] = kmt[:, pl.ds(0, 8), :]

    pl.semaphore_wait(barrier, 11)

    def send(src, dst, ssem, rsem, r, c):
        return pltpu.make_async_remote_copy(
            src_ref=src, dst_ref=dst, send_sem=send_sem.at[ssem], recv_sem=rsem, device_id={"row": r, "col": c}, device_id_type=MESH)

    own_rows = aligned(PAD + ROWS * row, ROWS)
    south, north = jnp.maximum(row - 1, 0), jnp.minimum(row + 1, 3)
    to_w = send(col_w, rcv_e, 0, edge_sem.at[0], row, west_col)
    to_e = send(col_e, rcv_w, 1, edge_sem.at[1], row, east_col)
    to_s = send(row_s, rcv_n, 2, edge_sem.at[2], south, col)
    to_n = send(row_n, rcv_s, 3, edge_sem.at[3], north, col)
    to_nw = send(col_w.at[V], rcv_se, 4, edge_sem.at[4], north, west_col)
    to_se = send(col_e.at[U], rcv_nw, 5, edge_sem.at[5], south, east_col)
    to_w.start()
    to_e.start()

    @pl.when(has_s)
    def _():
        to_s.start()
        to_se.start()

    @pl.when(has_n)
    def _():
        to_n.start()
        to_nw.start()

    def exchange(stg, stg_w, stg_e, first, count, base, rsem, esem, wsem, pe, pw):
        out = []
        for d, r in enumerate(peers):
            out.append(send(stg.at[r % 2], frame.at[pl.ds(first, count), OWN, own_rows, :], base + d, rsem.at[row], r, col))
        for r in range(4):
            out.append(send(stg_w.at[r % 2], pe.at[row], base + 3 + 2 * r, esem.at[row], r, west_col))
            out.append(send(stg_e.at[r % 2], pw.at[row], base + 4 + 2 * r, wsem.at[row], r, east_col))
        for copy in out:
            copy.start()
        frame[pl.ds(first, count), OWN, own_rows, :] = stg[core]
        return out

    def collect(stg, stg_w, first, count, rsem, esem, wsem, pe, pw):
        for r in peers:
            rows = aligned(PAD + ROWS * r, ROWS)
            send(stg.at[0], frame.at[pl.ds(first, count), OWN, rows, :], 0, rsem.at[r], r, col).wait_recv()
        for r in range(4):
            send(stg_w.at[0], pe.at[r], 0, esem.at[r], r, east_col).wait_recv()
            send(stg_w.at[0], pw.at[r], 0, wsem.at[r], r, west_col).wait_recv()
        side = lax.broadcasted_iota(jnp.int32, (ROWS, 128), 1) // HALO
        for r in range(4):
            for j in range(count):
                frame[first + j, 2, pl.ds(PAD + ROWS * r, ROWS), :] = jnp.where(
                    side == 0, turn(pe[r], (128 - HALO * j) % 128), jnp.where(side == 3, turn(pw[r], (128 - HALO * j - HALO) % 128), 0.0))

    sent = exchange(stage, stage_w, stage_e, ETA, 4, 6, row_sem, e_sem, w_sem, pk_e, pk_w)

    to_w.wait_recv()
    to_e.wait_recv()

    @pl.when(has_n)
    def _():
        to_s.wait_recv()
        to_se.wait_recv()

    @pl.when(has_s)
    def _():
        to_n.wait_recv()
        to_nw.wait_recv()

    def unpack_rows(g, carry):
        below, above = rcv_s[:, :, aligned(8 * g), :], rcv_n[:, :, aligned(8 * g), :]
        for j in range(8):
            k, m = 4 * g + j // 2, j % 2
            cube[:, k, m, OWN, pl.ds(PAD - 1, 1), :] = below[:, :, j:j + 1, :]
            cube[:, k, m, OWN, pl.ds(PAD + ROWS, 1), :] = above[:, :, j:j + 1, :]
        return carry

    lax.fori_loop(0, L // 4, unpack_rows, 0)
    kmt[:, pl.ds(ROWS, 8), :] = rcv_n[0, :, pl.ds(2 * L, 8), :]
    for i in range(3):
        rs = pl.ds(8 * i, 8)
        wet = kmt[:, rs, :]
        halo = turn(rcv_e[0, 0], 128 - (3 * L + i))
        nuv[0, :, rs, :] = jnp.minimum(wet, east(jnp.concatenate([wet, halo[None]], axis=0), 2))
        nuv[1, :, rs, :] = jnp.minimum(wet, kmt[:, pl.ds(8 * i + 1, 8), :])

    def unpack(k, carry):
        for i in range(3):
            slot = L * i + k
            cube[:, k, :, 2, pl.ds(PAD + 8 * i, 8), :] = jnp.where(
                lane42 < 64, turn(rcv_e[...], lax.rem(128 - slot, 128)), turn(rcv_w[...], 127 - slot))
        cube[V, k, :, 2, pl.ds(0, PAD), :] = turn(rcv_se[...], 128 - 2 * L - k)
        cube[U, k, :, 2, pl.ds(PAD + ROWS, PAD), :] = turn(rcv_nw[...], 127 - k)
        return carry

    lax.fori_loop(0, L, unpack, 0)

    press = PRESS_SCALE / L
    pair = jnp.zeros((2, 8, 128), F32)

    def for_strips(body, init, reverse=False):
        def strip(s, carry):
            m = s // 3
            i = s - 3 * m
            rs = aligned(8 * i)

            def get(f, k, part, d=0):
                start = PAD + 8 * i + d
                return cube[f, k, m, part, pl.ds(start if d else pl.multiple_of(start, 8), 8), :]

            state, finish = init(m, rs)

            def block(b, state):
                for j in range(LEVEL_BLOCK):
                    k = b * LEVEL_BLOCK + j
                    state = body(L - 1 - k if reverse else k, m, rs, get, state)
                return state

            finish(m, rs, lax.fori_loop(0, L // LEVEL_BLOCK, block, state))
            return carry

        lax.fori_loop(0, 6, strip, 0)

    def momentum_init(m, rs):
        return (pair,) * 6, momentum_finish

    def momentum_finish(m, rs, state):
        sums[0, m, :, rs, :] = state[4]
        sums[1, m, :, rs, :] = state[5]

    def momentum(k, m, rs, get, state):
        cx, cy, eu, ev, gu_sum, gv_sum = state
        level = k.astype(F32)
        both = slice(0, 3)
        u, v, un, vs = get(U, k, both), get(V, k, both), get(U, k, both, 1), get(V, k, both, -1)
        rho = HALINE_CON * get(S, k, both) - THERM_EXP * get(T, k, both)
        dx = rho[OWN] - east(rho, 2)
        dy = rho[OWN] - (HALINE_CON * get(S, k, OWN, 1) - THERM_EXP * get(T, k, OWN, 1))
        vsum, usum = v + vs, u + un
        cx, cy = cx + dx, cy + dy
        gu = press * (cx - 0.5 * dx) - 0.5 * (u[OWN] * (east(u, 2) - west(u, 2))) - 0.125 * (
            (vsum[OWN] + east(vsum, 2)) * (un[OWN] - get(U, k, OWN, -1)))
        gv = press * (cy - 0.5 * dy) - 0.125 * ((usum[OWN] + west(usum, 2)) * (east(v, 2) - west(v, 2))) - 0.5 * (
            v[OWN] * (get(V, k, OWN, 1) - vs[OWN]))
        gu = jnp.where(nuv[0, :, rs, :] > level, gu, 0.0)
        gv = jnp.where(nuv[1, :, rs, :] > level, gv, 0.0)
        inverse = table[0, k]
        eu = (u[OWN] + gu + VISC_NUMBER * eu) * inverse
        ev = (v[OWN] + gv + VISC_NUMBER * ev) * inverse
        sol[U, k, m, :, rs, :] = eu
        sol[V, k, m, :, rs, :] = ev
        return cx, cy, eu, ev, gu_sum + gu, gv_sum + gv

    for_strips(momentum, momentum_init)

    collect(stage, stage_w, ETA, 4, row_sem, e_sem, w_sem, pk_e, pk_w)

    def coefficients(i, carry):
        rs = aligned(PAD + 8 * i)
        depth = frame[DEPTH, :, rs, :]
        depth_e = east(depth)
        depth_n = frame[DEPTH, :, pl.ds(PAD + 8 * i + 1, 8), :]
        wet = depth > 0.0
        coef[0, :, rs, :] = jnp.where(wet, WAVE_COURANT, 0.0)
        coef[1, :, rs, :] = jnp.where(wet & (depth_e > 0.0), 0.5 * (depth + depth_e), 0.0)
        coef[2, :, rs, :] = jnp.where(wet & (depth_n > 0.0), 0.5 * (depth + depth_n), 0.0)
        return carry

    lax.fori_loop(0, 12, coefficients, 0)

    for d in range(2):
        scale = coef[1 + d, OWN, own_rows, :] / (jnp.maximum(nuv[d], 1.0) * float(sub_count))
        for m in range(2):
            fstage[m, d] = scale * sums[d, m]
    pack_2d(fstage, 2, fstage_w, fstage_e)
    sent += exchange(fstage, fstage_w, fstage_e, FX, 2, 17, frow_sem, fe_sem, fw_sem, fpk_e, fpk_w)

    def back_init(m, rs):
        return (pair,) * 4, back_finish

    def back_finish(m, rs, state):
        for d in range(2):
            sums[d, m, :, rs, :] = state[2 + d] / jnp.maximum(nuv[d, :, rs, :], 1.0)

    def back(k, m, rs, get, state):
        x, total = list(state[:2]), list(state[2:])
        level = k.astype(F32)
        for d in range(2):
            e, n = sol[d, k, m, :, rs, :], nuv[d, :, rs, :]
            x[d] = e + table[1, k] * jnp.where(n > level + 1.0, x[d], e * table[2, k])
            sol[d, k, m, :, rs, :] = x[d]
            total[d] = total[d] + jnp.where(n > level, x[d], 0.0)
        return (*x, *total)

    for_strips(back, back_init, reverse=True)

    stores = []

    def store(f, dst):
        for lt in range(2):
            stores.append(pltpu.make_async_copy(sol.at[f, :, :, lt], dst.at[:, :, :, pl.ds(LANES * lt, LANES)], store_sem.at[2 * f + lt]))
            stores[-1].start()

    store(U, xu_hbm)
    store(V, xv_hbm)

    def tracer_init(m, rs):
        return (pair,) * 2, lambda *a: None

    def tracers(k, m, rs, get, state):
        level = k.astype(F32)
        u, v, vs = 0.5 * get(U, k, slice(0, 3)), 0.5 * get(V, k, OWN), 0.5 * get(V, k, OWN, -1)
        out = []
        for f, e in zip((T, S), state):
            t = get(f, k, slice(0, 3))
            fx = u * (t + east(t))
            t = t[OWN]
            b = t - fx[OWN] + west(fx, 2) - v * (t + get(f, k, OWN, 1)) + vs * (t + get(f, k, OWN, -1))
            b = jnp.where(kmt[:, rs, :] > level, b, 0.0)
            out.append((b + DIFF_NUMBER * e) * table[3, k])
            sol[f, k, m, :, rs, :] = out[-1]
        return tuple(out)

    for_strips(tracers, tracer_init)
    store(T, ct_hbm)
    store(S, cs_hbm)
    acc[...] = jnp.zeros(acc.shape, F32)

    collect(fstage, fstage_w, FX, 2, frow_sem, fe_sem, fw_sem, fpk_e, fpk_w)

    def subcycles(first, last, tiles):
        base = PAD + chip * (8 * (12 - tiles))

        def body(n, carry):
            def rows_of(t):
                return aligned(base + 8 * t)

            def eta_tile(t):
                rs = rows_of(t)
                u, v = frame[TX, :, rs, :], frame[TY, :, rs, :]
                div = (u - west(u)) + (v - frame[TY, :, pl.ds(base + 8 * t - 1, 8), :])
                eta = frame[ETA, :, rs, :] - coef[0, :, rs, :] * div
                frame[ETA, :, rs, :] = eta
                return u, v, WAVE_COURANT * eta

            last_row = iota((3, 8, 128), 1) == 7
            following = eta_tile(0)
            for t in range(tiles):
                u, v, e = following
                if t + 1 < tiles:
                    following = eta_tile(t + 1)
                else:
                    following = (None, None, WAVE_COURANT * frame[ETA, :, rows_of(tiles), :])
                e_n = jnp.where(last_row, pltpu.roll(following[2], 7, 1), pltpu.roll(e, 7, 1))
                rs = rows_of(t)
                frame[TX, :, rs, :] = u + frame[FX, :, rs, :] - coef[1, :, rs, :] * (east(e) - e)
                frame[TY, :, rs, :] = v + frame[FY, :, rs, :] - coef[2, :, rs, :] * (e_n - e)
            chip_rows = aligned(PAD + 2 * ROWS * chip, 2 * ROWS)
            acc[...] += weights[n] * frame[pl.ds(0, 3), OWN, chip_rows, :]
            return carry

        lax.fori_loop(first, last, body, 0)

    def tiles_at(n):
        return min(-(-(2 * ROWS + sub_count - n) // 16) * 2, 12)

    n = 0
    while n < sub_count:
        last = n
        while last < sub_count and tiles_at(last) == tiles_at(n):
            last += 1
        subcycles(n, last, tiles_at(n))
        n = last

    mine = aligned(ROWS * core, ROWS)
    theirs = aligned(ROWS * (1 - core), ROWS)
    result[...] = acc[:, :, theirs, :]
    swap = send(result, result_in, 28, swap_sem, row + 1 - 2 * core, col)
    swap.start()
    swap.wait_recv()
    for m in range(2):
        whole = jnp.where(core == m, acc[:, :, mine, :], result_in[...])
        for lt in range(2):
            ls = pl.ds(LANES * lt, LANES)
            eta_out[m, :, ls] = whole[ETA, lt]
            tx_out[m, :, ls] = whole[TX, lt]
            ty_out[m, :, ls] = whole[TY, lt]
            for d, out in enumerate((qu_out, qv_out)):
                depth = coef[1 + d, lt, own_rows, :]
                out[m, :, ls] = whole[TX + d, lt] / jnp.where(depth > 0.0, depth, 1.0) - sums[d, m, lt]
                nuv_out[d, :, ls] = nuv[d, lt]

    for copy in stores:
        copy.wait()
    to_w.wait_send()
    to_e.wait_send()

    @pl.when(has_s)
    def _():
        to_s.wait_send()
        to_se.wait_send()

    @pl.when(has_n)
    def _():
        to_n.wait_send()
        to_nw.wait_send()

    for copy in sent:
        copy.wait_send()
    swap.wait_send()


def final_kernel(level_count, xu, xv, ct, cs, qu, qv, nuv, wet, eta_in, tx_in, ty_in,
                 eta_out, tx_out, ty_out, u_out, v_out, t_out, s_out):
    ratio = sweep_constants(level_count, DIFF_NUMBER)[1]
    eta_out[...] = eta_in[...]
    tx_out[...] = tx_in[...]
    ty_out[...] = ty_in[...]
    for lt in range(2):
        ls = pl.ds(LANES * lt, LANES)
        n_wet = wet[:, ls]
        for src, out in ((ct, t_out), (cs, s_out)):
            x = jnp.zeros(TILE, F32)
            for k in reversed(range(level_count)):
                e = src[k, 0, :, ls]
                x = e + ratio[k] * jnp.where(n_wet > k + 1, x, e * (1.0 / (1.0 - ratio[k])))
                out[k, 0, :, ls] = jnp.where(n_wet > k, x, 0.0)
        for d, (src, q, out) in enumerate(((xu, qu, u_out), (xv, qv, v_out))):
            n, mean = nuv[d, :, ls], q[0, :, ls]
            for k in range(level_count):
                out[k, 0, :, ls] = jnp.where(n > float(k), src[k, 0, :, ls] + mean, 0.0)


def solution(mesh):
    col_count = mesh.shape["col"]

    def local_step(vel_x, vel_y, pot_temp, salinity, surf_eta, trans_x, trans_y, col_depth, wet_levels, avg_weights):
        L = vel_x.shape[0]
        N = avg_weights.shape[0]
        any_spec = pl.BlockSpec(memory_space=pl.ANY)
        vmem_spec = pl.BlockSpec(memory_space=pltpu.VMEM)
        cube = jax.ShapeDtypeStruct(vel_x.shape, F32)
        flat = jax.ShapeDtypeStruct(surf_eta.shape, F32)
        vm = lambda *shape: pltpu.VMEM(shape, F32)
        dma = lambda n: pltpu.SemaphoreType.DMA((n,))
        inverse, ratio = sweep_constants(L, VISC_NUMBER)
        table = jnp.array([inverse, ratio, [1.0 / (1.0 - r) for r in ratio], sweep_constants(L, DIFF_NUMBER)[0]], F32)
        xu, xv, ct, cs, qu, qv, nuv, eta_o, tx_o, ty_o = pl.pallas_call(
            functools.partial(step_kernel, col_count, L, N),
            out_shape=[cube] * 4 + [flat] * 3 + [flat] * 3,
            in_specs=[any_spec] * 4 + [vmem_spec] * 5 + [pl.BlockSpec(memory_space=pltpu.SMEM)] * 2,
            out_specs=[any_spec] * 4 + [vmem_spec] * 6,
            scratch_shapes=[
                vm(4, L, M, RING, XR, LANES), vm(4, L, M, M, ROWS, LANES), *[vm(4, M, 8, LANES)] * 4, *[vm(4, M, M * L + 8, LANES)] * 4,
                *[vm(M, 8, LANES)] * 2, vm(M, ROWS + 8, LANES), vm(M, M, ROWS, LANES), vm(M, M, M, ROWS, LANES),
                vm(M, 4, M, ROWS, LANES), *[vm(M, ROWS, LANES)] * M, *[vm(4, ROWS, LANES)] * M,
                vm(M, M, M, ROWS, LANES), *[vm(M, ROWS, LANES)] * M, *[vm(4, ROWS, LANES)] * M,
                vm(6, RING, FRAME, LANES), vm(RING, RING, FRAME, LANES), vm(RING, M, M * ROWS, LANES), *[vm(RING, M, ROWS, LANES)] * M,
                dma(8), dma(8), dma(29), dma(6), *[dma(4)] * 6, pltpu.SemaphoreType.DMA],
            compiler_params=pltpu.CompilerParams(collective_id=0, has_side_effects=True),
            name="ocean_step",
        )(vel_x, vel_y, pot_temp, salinity, surf_eta, trans_x, trans_y, col_depth, wet_levels, avg_weights, table)
        cube_spec = pl.BlockSpec((L, 1, 8, 256), lambda m, i: (0, m, i, 0))
        flat_spec = pl.BlockSpec((1, 8, 256), lambda m, i: (m, i, 0))
        outs = pl.pallas_call(
            functools.partial(final_kernel, L),
            grid=(2, 3),
            out_shape=[flat] * 3 + [cube] * 4,
            in_specs=[cube_spec] * 4 + [flat_spec] * 2
            + [pl.BlockSpec((2, 8, 256), lambda m, i: (0, i, 0)), pl.BlockSpec((8, 256), lambda m, i: (i, 0))] + [flat_spec] * 3,
            out_specs=[flat_spec] * 3 + [cube_spec] * 4,
            name="ocean_final",
        )(xu, xv, ct, cs, qu, qv, nuv, wet_levels, eta_o, tx_o, ty_o)
        return tuple(outs)

    spec_3d = P(None, None, "row", "col")
    spec_2d = P(None, "row", "col")
    spec_map = P("row", "col")
    return jax.shard_map(local_step, mesh=mesh, in_specs=(spec_3d,) * 4 + (spec_2d,) * 3 + (spec_map,) * 2 + (P(),),
                         out_specs=(spec_2d,) * 3 + (spec_3d,) * 4, check_vma=False)
```

profile of v0, /device:TPU:0, one launch (start us, length us, event | category | flops | bytes accessed | tf_op | source)
XLA Modules:
  0.0 62.0 jit_solution(2543817888474902395)
XLA Ops:
  0.6 53.7 %ocean_step.1 = (f32[36,2,24,256]{3,2,1,0:T(8,128)}, f32[36,2,24,256]{3,2,1,0:T(8,128)}, f32[36,2,24,256]{3,2,1,0:T(8,128)}, f32[36,2,24,256]{3,2,1,0:T(8,128)},...) custom-call(f32[36,2,24,256]{3,2,1,0:T(8,128)} %u_hbm.1, ...), custom_call_target="tpu_custom_call" | custom-call | tf_op jit(solution)/shard_map/ocean_step/pallas_call | solution.py:527
  54.3 7.7 %ocean_final.1 = (f32[2,24,256]{2,1,0:T(8,128)}, f32[2,24,256]{2,1,0:T(8,128)}, f32[2,24,256]{2,1,0:T(8,128)}, f32[36,2,24,256]{3,2,1,0:T(8,128)}, f32[36,2,24,2...) custom-call(f32[36,2,24,256]{3,2,1,0:T(8,128)} %get-tuple-element.17.xu, ...), custom_call_target="tpu_custom_call" | custom-call | tf_op jit(solution)/shard_map/ocean_final/pallas_call | solution.py:544
where the time goes:
time: 62.4 us; the launch traced here: 62 us
  Pallas kernels  61.4 us (98%)
  between operations  0.64 us (1%)
    pallas_call x1, Pallas kernels, local_step(): pl.pallas_call(functools.partial(step_kernel, col_count, L, N), out_shape...  53.7 us
    pallas_call x1, Pallas kernels, local_step(): pl.pallas_call(functools.partial(final_kernel, L), grid=(2, 3), out_shape...  7.71 us

commit v1 on v0

--- a/solution.py
+++ b/solution.py
@@ -19,7 +19,8 @@
 ROWS = 24
 PAD = 8
 XR = ROWS + 2 * PAD
-LEVEL_BLOCK = 4
+EDGE_BLOCK = 4
+LEVEL_BLOCK = 12
 LANES = 128
 TILE = (8, LANES)
 RING = 3
@@ -145,9 +146,9 @@
 
     lane42 = lanes(4, 2)
 
-    def pack(k, carry):
+    def pack(g, carry):
         west_pack, east_pack = carry
-        for i in range(3):
+        for k, i in [(EDGE_BLOCK * g + j, i) for j in range(EDGE_BLOCK) for i in range(3)]:
             slot = L * i + k
             rs = pl.ds(PAD + 8 * i, 8)
             west_pack = jnp.where(lane42 == slot, turn(cube[:, k, :, 0, rs, :], slot), west_pack)
@@ -155,7 +156,7 @@
         return west_pack, east_pack
 
     empty = jnp.zeros((4, 2, 8, 128), F32)
-    west_pack, east_pack = lax.fori_loop(0, L, pack, (empty, empty))
+    west_pack, east_pack = lax.fori_loop(0, L // EDGE_BLOCK, pack, (empty, empty))
     col_w[...] = west_pack
     col_e[...] = east_pack
     for i in range(3):
@@ -263,16 +264,18 @@
         nuv[0, :, rs, :] = jnp.minimum(wet, east(jnp.concatenate([wet, halo[None]], axis=0), 2))
         nuv[1, :, rs, :] = jnp.minimum(wet, kmt[:, pl.ds(8 * i + 1, 8), :])
 
-    def unpack(k, carry):
-        for i in range(3):
-            slot = L * i + k
-            cube[:, k, :, 2, pl.ds(PAD + 8 * i, 8), :] = jnp.where(
-                lane42 < 64, turn(rcv_e[...], lax.rem(128 - slot, 128)), turn(rcv_w[...], 127 - slot))
-        cube[V, k, :, 2, pl.ds(0, PAD), :] = turn(rcv_se[...], 128 - 2 * L - k)
-        cube[U, k, :, 2, pl.ds(PAD + ROWS, PAD), :] = turn(rcv_nw[...], 127 - k)
+    def unpack(g, carry):
+        from_e, from_w = rcv_e[...], rcv_w[...]
+        for k in [EDGE_BLOCK * g + j for j in range(EDGE_BLOCK)]:
+            for i in range(3):
+                slot = L * i + k
+                cube[:, k, :, 2, pl.ds(PAD + 8 * i, 8), :] = jnp.where(
+                    lane42 < 64, turn(from_e, lax.rem(128 - slot, 128)), turn(from_w, 127 - slot))
+            cube[V, k, :, 2, pl.ds(0, PAD), :] = turn(rcv_se[...], 128 - 2 * L - k)
+            cube[U, k, :, 2, pl.ds(PAD + ROWS, PAD), :] = turn(rcv_nw[...], 127 - k)
         return carry
 
-    lax.fori_loop(0, L, unpack, 0)
+    lax.fori_loop(0, L // EDGE_BLOCK, unpack, 0)
 
     press = PRESS_SCALE / L
     pair = jnp.zeros((2, 8, 128), F32)

time: 62.4 us -> 51.5 us (0.83)
  Pallas kernels: 61.4 us -> 50.5 us
    pallas_call x1, Pallas kernels: 53.7 us -> 42.8 us  [local_step(): pl.pallas_call(functools.partial(step_kernel, col_count, L, N), out_shape...]
where the time goes in v1:
time: 51.5 us; the launch traced here: 51.1 us
  Pallas kernels  50.5 us (98%)
  between operations  0.64 us (1%)
    pallas_call x1, Pallas kernels, local_step(): pl.pallas_call(functools.partial(step_kernel, col_count, L, N), out_shape...  42.8 us
    pallas_call x1, Pallas kernels, local_step(): pl.pallas_call(functools.partial(final_kernel, L), grid=(2, 3), out_shape...  7.71 us

profile of v1, /device:TPU:0, one launch (start us, length us, event | category | flops | bytes accessed | tf_op | source)
XLA Modules:
  0.0 51.1 jit_solution(1449770575798253925)
XLA Ops:
  0.6 42.8 %ocean_step.1 = (f32[36,2,24,256]{3,2,1,0:T(8,128)}, f32[36,2,24,256]{3,2,1,0:T(8,128)}, f32[36,2,24,256]{3,2,1,0:T(8,128)}, f32[36,2,24,256]{3,2,1,0:T(8,128)},...) custom-call(f32[36,2,24,256]{3,2,1,0:T(8,128)} %u_hbm.1, ...), custom_call_target="tpu_custom_call" | custom-call | tf_op jit(solution)/shard_map/ocean_step/pallas_call | solution.py:530
  43.4 7.7 %ocean_final.1 = (f32[2,24,256]{2,1,0:T(8,128)}, f32[2,24,256]{2,1,0:T(8,128)}, f32[2,24,256]{2,1,0:T(8,128)}, f32[36,2,24,256]{3,2,1,0:T(8,128)}, f32[36,2,24,2...) custom-call(f32[36,2,24,256]{3,2,1,0:T(8,128)} %get-tuple-element.17.xu, ...), custom_call_target="tpu_custom_call" | custom-call | tf_op jit(solution)/shard_map/ocean_final/pallas_call | solution.py:547

commit v2 on v1

--- a/solution.py
+++ b/solution.py
@@ -25,6 +25,7 @@
 TILE = (8, LANES)
 RING = 3
 M = 2
+STEP_VMEM, FINAL_VMEM = 46 << 20, 8 << 20
 FRAME = 4 * ROWS + 2 * PAD
 HALO = 32
 
@@ -64,15 +65,16 @@
 def step_kernel(
     col_count, level_count, sub_count,
     u_hbm, v_hbm, t_hbm, s_hbm, eta_in, tx_in, ty_in, depth_in, wet_in, weights, table,
-    xu_hbm, xv_hbm, ct_hbm, cs_hbm, qu_out, qv_out, nuv_out, eta_out, tx_out, ty_out,
-    cube, sol,
+    sol_u, sol_v, sol_t, sol_s, qu_out, qv_out, nuv_out, eta_out, tx_out, ty_out,
+    cube,
     col_w, col_e, rcv_e, rcv_w, row_s, row_n, rcv_n, rcv_s, rcv_se, rcv_nw,
     kmt, nuv, sums, stage, stage_w, stage_e, pk_e, pk_w, fstage, fstage_w, fstage_e, fpk_e, fpk_w,
     frame, coef, acc, result, result_in,
-    load_sem, store_sem, send_sem, edge_sem, row_sem, e_sem, w_sem, frow_sem, fe_sem, fw_sem, swap_sem,
+    load_sem, send_sem, edge_sem, row_sem, e_sem, w_sem, frow_sem, fe_sem, fw_sem, swap_sem,
 ):
     L = level_count
     U, V, T, S = range(4)
+    sol = (sol_u, sol_v, sol_t, sol_s)
     ETA, TX, TY, DEPTH, FX, FY = range(6)
     OWN = slice(0, 2)
     col = lax.axis_index("col")
@@ -232,8 +234,6 @@
                 frame[first + j, 2, pl.ds(PAD + ROWS * r, ROWS), :] = jnp.where(
                     side == 0, turn(pe[r], (128 - HALO * j) % 128), jnp.where(side == 3, turn(pw[r], (128 - HALO * j - HALO) % 128), 0.0))
 
-    sent = exchange(stage, stage_w, stage_e, ETA, 4, 6, row_sem, e_sem, w_sem, pk_e, pk_w)
-
     to_w.wait_recv()
     to_e.wait_recv()
 
@@ -246,6 +246,8 @@
     def _():
         to_n.wait_recv()
         to_nw.wait_recv()
+
+    sent = exchange(stage, stage_w, stage_e, ETA, 4, 6, row_sem, e_sem, w_sem, pk_e, pk_w)
 
     def unpack_rows(g, carry):
         below, above = rcv_s[:, :, aligned(8 * g), :], rcv_n[:, :, aligned(8 * g), :]
@@ -329,8 +331,8 @@
         inverse = table[0, k]
         eu = (u[OWN] + gu + VISC_NUMBER * eu) * inverse
         ev = (v[OWN] + gv + VISC_NUMBER * ev) * inverse
-        sol[U, k, m, :, rs, :] = eu
-        sol[V, k, m, :, rs, :] = ev
+        sol[U][k, m, :, rs, :] = eu
+        sol[V][k, m, :, rs, :] = ev
         return cx, cy, eu, ev, gu_sum + gu, gv_sum + gv
 
     for_strips(momentum, momentum_init)
@@ -368,23 +370,13 @@
         x, total = list(state[:2]), list(state[2:])
         level = k.astype(F32)
         for d in range(2):
-            e, n = sol[d, k, m, :, rs, :], nuv[d, :, rs, :]
+            e, n = sol[d][k, m, :, rs, :], nuv[d, :, rs, :]
             x[d] = e + table[1, k] * jnp.where(n > level + 1.0, x[d], e * table[2, k])
-            sol[d, k, m, :, rs, :] = x[d]
+            sol[d][k, m, :, rs, :] = x[d]
             total[d] = total[d] + jnp.where(n > level, x[d], 0.0)
         return (*x, *total)
 
     for_strips(back, back_init, reverse=True)
-
-    stores = []
-
-    def store(f, dst):
-        for lt in range(2):
-            stores.append(pltpu.make_async_copy(sol.at[f, :, :, lt], dst.at[:, :, :, pl.ds(LANES * lt, LANES)], store_sem.at[2 * f + lt]))
-            stores[-1].start()
-
-    store(U, xu_hbm)
-    store(V, xv_hbm)
 
     def tracer_init(m, rs):
         return (pair,) * 2, lambda *a: None
@@ -400,12 +392,10 @@
             b = t - fx[OWN] + west(fx, 2) - v * (t + get(f, k, OWN, 1)) + vs * (t + get(f, k, OWN, -1))
             b = jnp.where(kmt[:, rs, :] > level, b, 0.0)
             out.append((b + DIFF_NUMBER * e) * table[3, k])
-            sol[f, k, m, :, rs, :] = out[-1]
+            sol[f][k, m, :, rs, :] = out[-1]
         return tuple(out)
 
     for_strips(tracers, tracer_init)
-    store(T, ct_hbm)
-    store(S, cs_hbm)
     acc[...] = jnp.zeros(acc.shape, F32)
 
     collect(fstage, fstage_w, FX, 2, frow_sem, fe_sem, fw_sem, fpk_e, fpk_w)
@@ -472,8 +462,6 @@
                 out[m, :, ls] = whole[TX + d, lt] / jnp.where(depth > 0.0, depth, 1.0) - sums[d, m, lt]
                 nuv_out[d, :, ls] = nuv[d, lt]
 
-    for copy in stores:
-        copy.wait()
     to_w.wait_send()
     to_e.wait_send()
 
@@ -492,25 +480,26 @@
     swap.wait_send()
 
 
-def final_kernel(level_count, xu, xv, ct, cs, qu, qv, nuv, wet, eta_in, tx_in, ty_in,
-                 eta_out, tx_out, ty_out, u_out, v_out, t_out, s_out):
+def final_kernel(level_count, sol_u, sol_v, sol_t, sol_s, qu, qv, nuv, wet, eta_in, tx_in, ty_in, eta_out, tx_out, ty_out, u_out, v_out, t_out, s_out):
     ratio = sweep_constants(level_count, DIFF_NUMBER)[1]
+    m = pl.program_id(0)
+    rs = pl.ds(pl.multiple_of(pl.program_id(1) * 8, 8), 8)
     eta_out[...] = eta_in[...]
     tx_out[...] = tx_in[...]
     ty_out[...] = ty_in[...]
     for lt in range(2):
         ls = pl.ds(LANES * lt, LANES)
         n_wet = wet[:, ls]
-        for src, out in ((ct, t_out), (cs, s_out)):
+        for src, out in ((sol_t, t_out), (sol_s, s_out)):
             x = jnp.zeros(TILE, F32)
             for k in reversed(range(level_count)):
-                e = src[k, 0, :, ls]
+                e = src[k, m, lt, rs, :]
                 x = e + ratio[k] * jnp.where(n_wet > k + 1, x, e * (1.0 / (1.0 - ratio[k])))
                 out[k, 0, :, ls] = jnp.where(n_wet > k, x, 0.0)
-        for d, (src, q, out) in enumerate(((xu, qu, u_out), (xv, qv, v_out))):
+        for d, (src, q, out) in enumerate(((sol_u, qu, u_out), (sol_v, qv, v_out))):
             n, mean = nuv[d, :, ls], q[0, :, ls]
             for k in range(level_count):
-                out[k, 0, :, ls] = jnp.where(n > float(k), src[k, 0, :, ls] + mean, 0.0)
+                out[k, 0, :, ls] = jnp.where(n > float(k), src[k, m, lt, rs, :] + mean, 0.0)
 
 
 def solution(mesh):
@@ -519,7 +508,7 @@
     def local_step(vel_x, vel_y, pot_temp, salinity, surf_eta, trans_x, trans_y, col_depth, wet_levels, avg_weights):
         L = vel_x.shape[0]
         N = avg_weights.shape[0]
-        any_spec = pl.BlockSpec(memory_space=pl.ANY)
+        hbm_spec = pl.BlockSpec(memory_space=pltpu.HBM)
         vmem_spec = pl.BlockSpec(memory_space=pltpu.VMEM)
         cube = jax.ShapeDtypeStruct(vel_x.shape, F32)
         flat = jax.ShapeDtypeStruct(surf_eta.shape, F32)
@@ -527,19 +516,19 @@
         dma = lambda n: pltpu.SemaphoreType.DMA((n,))
         inverse, ratio = sweep_constants(L, VISC_NUMBER)
         table = jnp.array([inverse, ratio, [1.0 / (1.0 - r) for r in ratio], sweep_constants(L, DIFF_NUMBER)[0]], F32)
-        xu, xv, ct, cs, qu, qv, nuv, eta_o, tx_o, ty_o = pl.pallas_call(
+        *sol, qu, qv, nuv, eta_o, tx_o, ty_o = pl.pallas_call(
             functools.partial(step_kernel, col_count, L, N),
-            out_shape=[cube] * 4 + [flat] * 3 + [flat] * 3,
-            in_specs=[any_spec] * 4 + [vmem_spec] * 5 + [pl.BlockSpec(memory_space=pltpu.SMEM)] * 2,
-            out_specs=[any_spec] * 4 + [vmem_spec] * 6,
+            out_shape=[jax.ShapeDtypeStruct((L, M, M, ROWS, LANES), F32)] * 4 + [flat] * 6,
+            in_specs=[hbm_spec] * 4 + [vmem_spec] * 5 + [pl.BlockSpec(memory_space=pltpu.SMEM)] * 2,
+            out_specs=[vmem_spec] * 10,
             scratch_shapes=[
-                vm(4, L, M, RING, XR, LANES), vm(4, L, M, M, ROWS, LANES), *[vm(4, M, 8, LANES)] * 4, *[vm(4, M, M * L + 8, LANES)] * 4,
+                vm(4, L, M, RING, XR, LANES), *[vm(4, M, 8, LANES)] * 4, *[vm(4, M, M * L + 8, LANES)] * 4,
                 *[vm(M, 8, LANES)] * 2, vm(M, ROWS + 8, LANES), vm(M, M, ROWS, LANES), vm(M, M, M, ROWS, LANES),
                 vm(M, 4, M, ROWS, LANES), *[vm(M, ROWS, LANES)] * M, *[vm(4, ROWS, LANES)] * M,
                 vm(M, M, M, ROWS, LANES), *[vm(M, ROWS, LANES)] * M, *[vm(4, ROWS, LANES)] * M,
                 vm(6, RING, FRAME, LANES), vm(RING, RING, FRAME, LANES), vm(RING, M, M * ROWS, LANES), *[vm(RING, M, ROWS, LANES)] * M,
-                dma(8), dma(8), dma(29), dma(6), *[dma(4)] * 6, pltpu.SemaphoreType.DMA],
-            compiler_params=pltpu.CompilerParams(collective_id=0, has_side_effects=True),
+                dma(8), dma(29), dma(6), *[dma(4)] * 6, pltpu.SemaphoreType.DMA],
+            compiler_params=pltpu.CompilerParams(collective_id=0, has_side_effects=True, vmem_limit_bytes=STEP_VMEM),
             name="ocean_step",
         )(vel_x, vel_y, pot_temp, salinity, surf_eta, trans_x, trans_y, col_depth, wet_levels, avg_weights, table)
         cube_spec = pl.BlockSpec((L, 1, 8, 256), lambda m, i: (0, m, i, 0))
@@ -548,11 +537,12 @@
             functools.partial(final_kernel, L),
             grid=(2, 3),
             out_shape=[flat] * 3 + [cube] * 4,
-            in_specs=[cube_spec] * 4 + [flat_spec] * 2
+            in_specs=[vmem_spec] * 4 + [flat_spec] * 2
             + [pl.BlockSpec((2, 8, 256), lambda m, i: (0, i, 0)), pl.BlockSpec((8, 256), lambda m, i: (i, 0))] + [flat_spec] * 3,
             out_specs=[flat_spec] * 3 + [cube_spec] * 4,
             name="ocean_final",
-        )(xu, xv, ct, cs, qu, qv, nuv, wet_levels, eta_o, tx_o, ty_o)
+            compiler_params=pltpu.CompilerParams(vmem_limit_bytes=FINAL_VMEM),
+        )(*sol, qu, qv, nuv, wet_levels, eta_o, tx_o, ty_o)
         return tuple(outs)
 
     spec_3d = P(None, None, "row", "col")

time: 51.5 us -> 51.5 us (level)
  Pallas kernels: 50.5 us -> 45.1 us
  local copies, waits for them, and re-layouts: 0 us -> 5.2 us
    unnamed x0 -> x14, local copies, waits for them, and re-layouts: none -> 5.2 us
    pallas_call x1, Pallas kernels: 7.71 us -> 3.97 us  [local_step(): pl.pallas_call(functools.partial(final_kernel, L), grid=(2, 3), out_shape...]
    pallas_call x1, Pallas kernels: 42.8 us -> 41.1 us  [local_step(): pl.pallas_call(functools.partial(step_kernel, col_count, L, N), out_shape...]
where the time goes in v2:
time: 51.5 us; the launch traced here: 50.9 us
  Pallas kernels  45.1 us (88%)
  local copies, waits for them, and re-layouts  5.2 us (10%)
  between operations  0.66 us (1%)
    pallas_call x1, Pallas kernels, local_step(): pl.pallas_call(functools.partial(step_kernel, col_count, L, N), out_shape...  41.1 us
    unnamed x14, local copies, waits for them, and re-layouts  5.2 us
    pallas_call x1, Pallas kernels, local_step(): pl.pallas_call(functools.partial(final_kernel, L), grid=(2, 3), out_shape...  3.97 us

profile of v2, /device:TPU:0, one launch (start us, length us, event | category | flops | bytes accessed | tf_op | source)
XLA Modules:
  0.0 50.9 jit_solution(10684537881906440570)
XLA Ops:
  0.6 0.0 copy-start
  0.6 0.7 %copy-done = s32[24,256]{1,0:T(8,128)S(1)} copy-done((s32[24,256]{1,0:T(8,128)S(1)}, s32[24,256]{1,0:T(8,128)}, u32[]{:S(2)}) %copy-start) | copy-done | bytes 24600
  1.4 0.0 copy-start.1
  1.4 0.8 %copy-done.1 = f32[2,24,256]{2,1,0:T(8,128)S(1)} copy-done((f32[2,24,256]{2,1,0:T(8,128)S(1)}, f32[2,24,256]{2,1,0:T(8,128)}, u32[]{:S(2)}) %copy-start.1) | copy-done | bytes 49176
  2.2 0.0 copy-start.2
  2.2 0.8 %copy-done.2 = f32[2,24,256]{2,1,0:T(8,128)S(1)} copy-done((f32[2,24,256]{2,1,0:T(8,128)S(1)}, f32[2,24,256]{2,1,0:T(8,128)}, u32[]{:S(2)}) %copy-start.2) | copy-done | bytes 49176
  3.0 0.0 copy-start.3
  3.0 0.8 %copy-done.3 = f32[2,24,256]{2,1,0:T(8,128)S(1)} copy-done((f32[2,24,256]{2,1,0:T(8,128)S(1)}, f32[2,24,256]{2,1,0:T(8,128)}, u32[]{:S(2)}) %copy-start.3) | copy-done | bytes 49176
  3.8 0.0 copy-start.4
  3.8 0.7 %copy-done.4 = f32[24,256]{1,0:T(8,128)S(1)} copy-done((f32[24,256]{1,0:T(8,128)S(1)}, f32[24,256]{1,0:T(8,128)}, u32[]{:S(2)}) %copy-start.4) | copy-done | bytes 24600
  4.5 0.0 copy-start.5
  4.5 0.7 %copy-done.5 = f32[4,36]{1,0:T(4,128)S(1)} copy-done((f32[4,36]{1,0:T(4,128)S(1)}, f32[4,36]{1,0:T(4,128)}, u32[]{:S(2)}) %copy-start.5) | copy-done | bytes 600
  5.2 0.0 copy-start.6
  5.2 0.7 %copy-done.6 = f32[30]{0:T(128)S(1)} copy-done((f32[30]{0:T(128)S(1)}, f32[30]{0:T(128)}, u32[]{:S(2)}) %copy-start.6) | copy-done | bytes 144
  5.8 41.1 %ocean_step.1 = (f32[36,2,2,24,128]{4,3,2,1,0:T(8,128)S(1)}, f32[36,2,2,24,128]{4,3,2,1,0:T(8,128)S(1)}, f32[36,2,2,24,128]{4,3,2,1,0:T(8,128)S(1)}, f32[36,2,2,...) custom-call(f32[36,2,24,256]{3,2,1,0:T(8,128)} %u_hbm.1, ...), custom_call_target="tpu_custom_call" | custom-call | tf_op jit(solution)/shard_map/ocean_step/pallas_call | solution.py:519
  46.9 4.0 %ocean_final.1 = (f32[2,24,256]{2,1,0:T(8,128)}, f32[2,24,256]{2,1,0:T(8,128)}, f32[2,24,256]{2,1,0:T(8,128)}, f32[36,2,24,256]{3,2,1,0:T(8,128)}, f32[36,2,24,2...) custom-call(f32[36,2,2,24,128]{4,3,2,1,0:T(8,128)S(1)} %get-tuple-element.17.sol_u, ...), custom_call_target="tpu_custom_call" | custom-call | tf_op jit(solution)/shard_map/ocean_final/pallas_call | solution.py:536
Async XLA Ops:
  0.6 0.7 %copy-start = (s32[24,256]{1,0:T(8,128)S(1)}, s32[24,256]{1,0:T(8,128)}, u32[]{:S(2)}) copy-start(s32[24,256]{1,0:T(8,128)} %wet.1) | copy-start | bytes 73732
  1.4 0.8 %copy-start.1 = (f32[2,24,256]{2,1,0:T(8,128)S(1)}, f32[2,24,256]{2,1,0:T(8,128)}, u32[]{:S(2)}) copy-start(f32[2,24,256]{2,1,0:T(8,128)} %eta_in.1) | copy-start | bytes 147460
  2.2 0.8 %copy-start.2 = (f32[2,24,256]{2,1,0:T(8,128)S(1)}, f32[2,24,256]{2,1,0:T(8,128)}, u32[]{:S(2)}) copy-start(f32[2,24,256]{2,1,0:T(8,128)} %tx_in.1) | copy-start | bytes 147460
  3.0 0.8 %copy-start.3 = (f32[2,24,256]{2,1,0:T(8,128)S(1)}, f32[2,24,256]{2,1,0:T(8,128)}, u32[]{:S(2)}) copy-start(f32[2,24,256]{2,1,0:T(8,128)} %ty_in.1) | copy-start | bytes 147460
  3.8 0.7 %copy-start.4 = (f32[24,256]{1,0:T(8,128)S(1)}, f32[24,256]{1,0:T(8,128)}, u32[]{:S(2)}) copy-start(f32[24,256]{1,0:T(8,128)} %depth_in.1) | copy-start | bytes 73732
  4.5 0.7 %copy-start.5 = (f32[4,36]{1,0:T(4,128)S(1)}, f32[4,36]{1,0:T(4,128)}, u32[]{:S(2)}) copy-start(f32[4,36]{1,0:T(4,128)} %constant.2.clone.table) | copy-start | bytes 1732
  5.2 0.7 %copy-start.6 = (f32[30]{0:T(128)S(1)}, f32[30]{0:T(128)}, u32[]{:S(2)}) copy-start(f32[30]{0:T(128)} %weights.1) | copy-start | bytes 364

commit v3 on v2

v3 whole, which is shorter than its diff:
```python
import functools

import jax
import jax.numpy as jnp
from jax import lax
from jax.experimental import pallas as pl
from jax.experimental.pallas import tpu as pltpu
from jax.sharding import PartitionSpec as P

WAVE_COURANT = 0.4
THERM_EXP = 0.2
HALINE_CON = 0.15
PRESS_SCALE = 0.5
VISC_NUMBER = 1.0
DIFF_NUMBER = 0.5

MESH = pl.DeviceIdType.MESH
F32 = jnp.float32
ROWS = 24
PAD = 8
XR = ROWS + 2 * PAD
EDGE_BLOCK = 4
LEVEL_BLOCK = 12
LANES = 128
SUB = 8
TILE = (SUB, LANES)
PAIR, STRIPS, QUAD, OCTET = range(2), range(3), range(4), range(SUB)
RING = 3
M = 2
STEP_VMEM, FINAL_VMEM = 46 << 20, 8 << 20
FRAME = 4 * ROWS + 2 * PAD
HALO = 32


def sweep_constants(level_count, strength):
    inverse, ratio = [], []
    for k in range(level_count):
        pivot = 1.0 + strength if k == 0 else 1.0 + 2.0 * strength - strength * ratio[-1]
        inverse.append(1.0 / pivot)
        ratio.append(strength / pivot)
    return inverse, ratio


def iota(shape, axis):
    return lax.broadcasted_iota(jnp.int32, shape, axis)


def lanes(*lead):
    return iota((*lead, 8, 128), len(lead) + 1)


def turn(x, shift):
    return pltpu.roll(x, shift, x.ndim - 1)


def east(x):
    rolled = turn(x, 127)
    return jnp.where(lanes(3) == 127, jnp.concatenate([rolled[1:], rolled[:1]], axis=0), rolled)


def west(x):
    rolled = turn(x, 1)
    return jnp.where(lanes(3) == 0, jnp.concatenate([rolled[2:], rolled[:2]], axis=0), rolled)


def east_block(x):
    rolled = turn(x[:2], 127)
    return jnp.where(lanes(2) == 127, jnp.concatenate([rolled[1:], x[2:]], axis=0), rolled)


def west_block(x):
    rolled = turn(x[:2], 1)
    return jnp.where(lanes(2) == 0, jnp.concatenate([x[2:], rolled[:1]], axis=0), rolled)


ETA, TX, TY, DEPTH, PACK, KMT = range(6)


def pack_2d(stage, count, put):
    lane = lanes()
    for i in STRIPS:
        rs = pl.ds(SUB * i, SUB)
        for m in PAIR:
            pack_w = pack_e = jnp.zeros(TILE, F32)
            for j in range(count):
                here = lane // HALO == j
                pack_w = jnp.where(here, turn(stage[m, j, 0, rs, :], HALO * j), pack_w)
                pack_e = jnp.where(here, turn(stage[m, j, 1, rs, :], (HALO * j + HALO) % LANES), pack_e)
            put(m, rs, pack_w, pack_e)


def stage_kernel(sub_count, eta, tx, ty, depth, wet_in, weights, stage):
    for lt in PAIR:
        ls = pl.ds(LANES * lt, LANES)
        wet = wet_in[:, ls].astype(F32)
        masked = jnp.where(wet > 0.0, depth[:, ls], 0.0)
        stage[0, KMT, lt] = wet
        for m in PAIR:
            for j, field in ((ETA, eta), (TX, tx), (TY, ty)):
                stage[m, j, lt] = field[m, :, ls]
            stage[m, DEPTH, lt] = masked
    for n in range(sub_count):
        stage[1, KMT, n // ROWS, pl.ds(n % ROWS, 1), :] = jnp.full((1, LANES), weights[n], F32)

    def put(m, rs, pack_w, pack_e):
        stage[m, PACK, 0, rs, :] = pack_w
        stage[m, PACK, 1, rs, :] = pack_e

    pack_2d(stage, 4, put)


def step_kernel(
    col_count, level_count, sub_count,
    u_hbm, v_hbm, t_hbm, s_hbm, stage,
    sol_u, sol_v, sol_t, sol_s, qu_out, qv_out, nuv_out, eta_out, tx_out, ty_out,
    cube,
    col_w, col_e, rcv_e, rcv_w, row_s, row_n, rcv_n, rcv_s, rcv_se, rcv_nw,
    kmt, nuv, sums, pk_e, pk_w, fstage, fstage_w, fstage_e, fpk_e, fpk_w,
    frame, coef, acc, result, result_in,
    table, load_sem, send_sem, edge_sem, row_sem, e_sem, w_sem, frow_sem, fe_sem, fw_sem, swap_sem,
):
    L = level_count
    U, V, T, S = range(4)
    sol = (sol_u, sol_v, sol_t, sol_s)
    FX, FY = 4, 5
    OWN = slice(0, 2)
    col = lax.axis_index("col")
    row = lax.axis_index("row")
    chip = row // 2
    core = row % 2
    east_col = lax.rem(col + 1, col_count)
    west_col = lax.rem(col + col_count - 1, col_count)
    peers = [lax.rem(row + d, 4) for d in (1, 2, 3)]
    lane = lanes()
    zero = jnp.zeros(TILE, F32)

    def aligned(start, size=8):
        return pl.ds(pl.multiple_of(start, 8), size)

    barrier = pltpu.get_barrier_semaphore()
    for r in peers:
        pl.semaphore_signal(barrier, inc=1, device_id={"row": r, "col": col}, device_id_type=MESH)
    for other in (east_col, west_col):
        for r in QUAD:
            pl.semaphore_signal(barrier, inc=1, device_id={"row": r, "col": other}, device_id_type=MESH)

    loads = []
    for f, src in enumerate((u_hbm, v_hbm, t_hbm, s_hbm)):
        for lt in PAIR:
            loads.append(pltpu.make_async_copy(
                src.at[:, :, :, pl.ds(LANES * lt, LANES)], cube.at[f, :, :, lt, pl.ds(PAD, ROWS), :], load_sem.at[2 * f + lt]))
            loads[-1].start()

    inv_v, ratio_v = sweep_constants(L, VISC_NUMBER)
    for n, line in enumerate((inv_v, ratio_v, [1.0 / (1.0 - r) for r in ratio_v], sweep_constants(L, DIFF_NUMBER)[0])):
        for k in range(L):
            table[n, k] = line[k]

    kmt[:, pl.ds(0, ROWS), :] = stage[0, KMT]

    has_s, has_n = row > 0, row < 3

    @pl.when(row == 0)
    def _():
        rcv_s[...] = jnp.zeros(rcv_s.shape, F32)
        rcv_se[...] = jnp.zeros(rcv_se.shape, F32)

    @pl.when(row == 3)
    def _():
        rcv_n[...] = jnp.zeros(rcv_n.shape, F32)
        rcv_nw[...] = jnp.zeros(rcv_nw.shape, F32)

    frame[:, :, pl.ds(0, PAD), :] = jnp.zeros((6, 3, PAD, 128), F32)
    frame[:, :, pl.ds(PAD + 4 * ROWS, PAD), :] = jnp.zeros((6, 3, PAD, 128), F32)

    for copy in loads:
        copy.wait()

    lane42 = lanes(4, 2)

    def pack(g, carry):
        west_pack, east_pack = carry
        for k, i in [(EDGE_BLOCK * g + j, i) for j in range(EDGE_BLOCK) for i in STRIPS]:
            slot = L * i + k
            rs = pl.ds(PAD + SUB * i, SUB)
            west_pack = jnp.where(lane42 == slot, turn(cube[:, k, :, 0, rs, :], slot), west_pack)
            east_pack = jnp.where(lane42 == slot, turn(cube[:, k, :, 1, rs, :], slot + 1), east_pack)
        return west_pack, east_pack

    empty = jnp.zeros((4, M, SUB, LANES), F32)
    west_pack, east_pack = lax.fori_loop(0, L // EDGE_BLOCK, pack, (empty, empty))
    col_w[...] = west_pack
    col_e[...] = east_pack
    for i in STRIPS:
        slot = 3 * L + i
        col_w[0, 0] = jnp.where(lane == slot, turn(kmt[0, pl.ds(SUB * i, SUB), :], slot), col_w[0, 0])

    sub42 = iota((4, M, SUB, LANES), 2)

    def pack_rows(g, carry):
        low = high = empty
        for j in OCTET:
            k, m = 4 * g + j // 2, j % 2
            low = jnp.where(sub42 == j, cube[:, k, m, OWN, pl.ds(PAD - j, 8), :], low)
            high = jnp.where(sub42 == j, cube[:, k, m, OWN, pl.ds(PAD + ROWS - 1 - j, 8), :], high)
        rows = aligned(SUB * g)
        row_s[:V + 1, :, rows, :] = low[:T]
        row_s[T, :, rows, :] = low[T] - (HALINE_CON / THERM_EXP) * low[S]
        row_s[S:, :, rows, :] = low[T:]
        row_n[:, :, rows, :] = high
        return carry

    lax.fori_loop(0, L // 4, pack_rows, 0)
    row_s[U, :, pl.ds(M * L, SUB), :] = kmt[:, pl.ds(0, SUB), :]

    pl.semaphore_wait(barrier, 11)

    def send(src, dst, ssem, rsem, r, c):
        return pltpu.make_async_remote_copy(
            src_ref=src, dst_ref=dst, send_sem=send_sem.at[ssem], recv_sem=rsem, device_id={"row": r, "col": c}, device_id_type=MESH)

    own_rows = aligned(PAD + ROWS * row, ROWS)
    south, north = jnp.maximum(row - 1, 0), jnp.minimum(row + 1, 3)
    to_w = send(col_w, rcv_e, 0, edge_sem.at[0], row, west_col)
    to_e = send(col_e, rcv_w, 1, edge_sem.at[1], row, east_col)
    first_s, first_n = pl.ds(0, 3), pl.ds(0, 2)
    later_s, later_n = pl.ds(3, 2), pl.ds(2, 2)
    to_s = send(row_s.at[first_s], rcv_n.at[first_s], 2, edge_sem.at[2], south, col)
    to_n = send(row_n.at[first_n], rcv_s.at[first_n], 3, edge_sem.at[3], north, col)
    to_s_later = send(row_s.at[later_s], rcv_n.at[later_s], 6, edge_sem.at[6], south, col)
    to_n_later = send(row_n.at[later_n], rcv_s.at[later_n], 7, edge_sem.at[7], north, col)
    to_nw = send(col_w.at[V], rcv_se, 4, edge_sem.at[4], north, west_col)
    to_se = send(col_e.at[U], rcv_nw, 5, edge_sem.at[5], south, east_col)
    to_w.start()
    to_e.start()

    @pl.when(has_s)
    def _():
        to_s.start()
        to_se.start()
        to_s_later.start()

    @pl.when(has_n)
    def _():
        to_n.start()
        to_nw.start()
        to_n_later.start()

    def exchange(block, pack_w, pack_e, first, count, base, rsem, esem, wsem, pe, pw):
        out = []
        for d, r in enumerate(peers):
            out.append(send(block(r % 2), frame.at[pl.ds(first, count), OWN, own_rows, :], base + d, rsem.at[row], r, col))
        for r in QUAD:
            out.append(send(pack_w(r % 2), pe.at[row], base + 3 + 2 * r, esem.at[row], r, west_col))
            out.append(send(pack_e(r % 2), pw.at[row], base + 4 + 2 * r, wsem.at[row], r, east_col))
        for copy in out:
            copy.start()
        frame[pl.ds(first, count), OWN, own_rows, :] = block(core)[...]
        return out

    def collect(block, pack_w, first, count, rsem, esem, wsem, pe, pw):
        for r in peers:
            rows = aligned(PAD + ROWS * r, ROWS)
            send(block(0), frame.at[pl.ds(first, count), OWN, rows, :], 0, rsem.at[r], r, col).wait_recv()
        for r in QUAD:
            send(pack_w(0), pe.at[r], 0, esem.at[r], r, east_col).wait_recv()
            send(pack_w(0), pw.at[r], 0, wsem.at[r], r, west_col).wait_recv()
        side = lax.broadcasted_iota(jnp.int32, (ROWS, 128), 1) // HALO
        for r in QUAD:
            for j in range(count):
                frame[first + j, 2, pl.ds(PAD + ROWS * r, ROWS), :] = jnp.where(
                    side == 0, turn(pe[r], (128 - HALO * j) % 128), jnp.where(side == 3, turn(pw[r], (128 - HALO * j - HALO) % 128), 0.0))

    def stage_block(m):
        return stage.at[m, pl.ds(0, PACK)]

    def stage_w(m):
        return stage.at[m, PACK, 0]

    def stage_e(m):
        return stage.at[m, PACK, 1]

    to_w.wait_recv()
    to_e.wait_recv()

    def unpack(g, carry):
        from_e, from_w = rcv_e[...], rcv_w[...]
        for k in [EDGE_BLOCK * g + j for j in range(EDGE_BLOCK)]:
            for i in STRIPS:
                slot = L * i + k
                cube[:, k, :, 2, pl.ds(PAD + SUB * i, SUB), :] = jnp.where(
                    lane42 < 64, turn(from_w, lax.rem(128 - slot, 128)), turn(from_e, 127 - slot))
        return carry

    lax.fori_loop(0, L // EDGE_BLOCK, unpack, 0)

    def masks(i):
        rs = pl.ds(SUB * i, SUB)
        wet = kmt[:, rs, :]
        halo = turn(rcv_e[0, 0], 127 - (3 * L + i))
        nuv[0, :, rs, :] = jnp.minimum(wet, east_block(jnp.concatenate([wet, halo[None]], axis=0)))
        nuv[1, :, rs, :] = jnp.minimum(wet, kmt[:, pl.ds(8 * i + 1, 8), :])

    masks(0)
    masks(1)

    press = PRESS_SCALE / L
    pair = jnp.zeros((M, SUB, LANES), F32)

    def for_strips(body, init, reverse=False, strips=(0, 1, 3)):
        start, step, count = strips

        def strip(s, carry):
            m = s // count
            i = start + step * (s - count * m)
            rs = aligned(SUB * i)

            def get(f, k, part, d=0):
                start = PAD + 8 * i + d
                return cube[f, k, m, part, pl.ds(start if d else pl.multiple_of(start, 8), 8), :]

            state, finish = init(m, rs)

            def block(b, state):
                for j in range(LEVEL_BLOCK):
                    k = b * LEVEL_BLOCK + j
                    state = body(L - 1 - k if reverse else k, m, rs, get, state)
                return state

            finish(m, rs, lax.fori_loop(0, L // LEVEL_BLOCK, block, state))
            return carry

        lax.fori_loop(0, M * count, strip, 0)

    def momentum_init(m, rs):
        return (pair,) * 6, momentum_finish

    def momentum_finish(m, rs, state):
        sums[0, m, :, rs, :] = state[4]
        sums[1, m, :, rs, :] = state[5]

    def momentum(k, m, rs, get, state):
        cx, cy, eu, ev, gu_sum, gv_sum = state
        level = k.astype(F32)
        both = slice(0, 3)
        u, v, un, vs = get(U, k, both), get(V, k, both), get(U, k, both, 1), get(V, k, both, -1)
        rho = HALINE_CON * get(S, k, both) - THERM_EXP * get(T, k, both)
        dx = rho[OWN] - east_block(rho)
        dy = rho[OWN] - (HALINE_CON * get(S, k, OWN, 1) - THERM_EXP * get(T, k, OWN, 1))
        vsum, usum = v + vs, u + un
        cx, cy = cx + dx, cy + dy
        gu = press * (cx - 0.5 * dx) - 0.5 * (u[OWN] * (east_block(u) - west_block(u))) - 0.125 * (
            (vsum[OWN] + east_block(vsum)) * (un[OWN] - get(U, k, OWN, -1)))
        gv = press * (cy - 0.5 * dy) - 0.125 * ((usum[OWN] + west_block(usum)) * (east_block(v) - west_block(v))) - 0.5 * (
            v[OWN] * (get(V, k, OWN, 1) - vs[OWN]))
        gu = jnp.where(nuv[0, :, rs, :] > level, gu, 0.0)
        gv = jnp.where(nuv[1, :, rs, :] > level, gv, 0.0)
        inverse = table[0, k]
        eu = (u[OWN] + gu + VISC_NUMBER * eu) * inverse
        ev = (v[OWN] + gv + VISC_NUMBER * ev) * inverse
        sol[U][k, m, :, rs, :] = eu
        sol[V][k, m, :, rs, :] = ev
        return cx, cy, eu, ev, gu_sum + gu, gv_sum + gv

    for_strips(momentum, momentum_init, strips=(1, 1, 1))

    @pl.when(has_n)
    def _():
        to_s.wait_recv()
        to_se.wait_recv()

    @pl.when(has_s)
    def _():
        to_n.wait_recv()
        to_nw.wait_recv()

    sent = exchange(stage_block, stage_w, stage_e, ETA, 4, 8, row_sem, e_sem, w_sem, pk_e, pk_w)

    def unpack_rows(g, carry):
        rows = aligned(SUB * g)
        below, above = rcv_s[:T, :, rows, :], rcv_n[:S, :, rows, :]
        for j in OCTET:
            k, m = 4 * g + j // 2, j % 2
            cube[:T, k, m, OWN, pl.ds(PAD - 1, 1), :] = below[:, :, j:j + 1, :]
            cube[:S, k, m, OWN, pl.ds(PAD + ROWS, 1), :] = above[:, :, j:j + 1, :]
            cube[S, k, m, OWN, pl.ds(PAD + ROWS, 1), :] = jnp.zeros((M, 1, LANES), F32)
            if m:
                cube[V, k, :, 2, pl.ds(0, PAD), :] = turn(rcv_se[...], 127 - 2 * L - k)
                cube[U, k, :, 2, pl.ds(PAD + ROWS, PAD), :] = turn(rcv_nw[...], lax.rem(128 - k, 128))
        return carry

    def unpack_rows_later(g, carry):
        rows = aligned(SUB * g)
        below, above = rcv_s[T:, :, rows, :], rcv_n[S:, :, rows, :]
        for j in OCTET:
            k, m = 4 * g + j // 2, j % 2
            cube[T:, k, m, OWN, pl.ds(PAD - 1, 1), :] = below[:, :, j:j + 1, :]
            cube[T:, k, m, OWN, pl.ds(PAD + ROWS, 1), :] = above[:, :, j:j + 1, :]
        return carry

    lax.fori_loop(0, L // 4, unpack_rows, 0)
    kmt[:, pl.ds(ROWS, 8), :] = rcv_n[U, :, pl.ds(M * L, SUB), :]
    masks(2)
    for_strips(momentum, momentum_init, strips=(0, 2, 2))

    collect(stage_block, stage_w, ETA, 4, row_sem, e_sem, w_sem, pk_e, pk_w)

    def coefficients(i, carry):
        rs = aligned(PAD + 8 * i)
        depth = frame[DEPTH, :, rs, :]
        depth_e = east(depth)
        depth_n = frame[DEPTH, :, pl.ds(PAD + 8 * i + 1, 8), :]
        wet = depth > 0.0
        coef[0, :, rs, :] = jnp.where(wet, WAVE_COURANT, 0.0)
        coef[1, :, rs, :] = jnp.where(wet & (depth_e > 0.0), 0.5 * (depth + depth_e), 0.0)
        coef[2, :, rs, :] = jnp.where(wet & (depth_n > 0.0), 0.5 * (depth + depth_n), 0.0)
        return carry

    lax.fori_loop(0, 12, coefficients, 0)

    for d in PAIR:
        scale = coef[1 + d, OWN, own_rows, :] / (jnp.maximum(nuv[d], 1.0) * float(sub_count))
        for m in PAIR:
            fstage[m, d] = scale * sums[d, m]

    def put(m, rs, pack_w, pack_e):
        fstage_w[m, rs, :] = pack_w
        fstage_e[m, rs, :] = pack_e

    pack_2d(fstage, 2, put)
    sent += exchange(lambda m: fstage.at[m], lambda m: fstage_w.at[m], lambda m: fstage_e.at[m], FX, 2, 19, frow_sem, fe_sem, fw_sem, fpk_e, fpk_w)

    def back_init(m, rs):
        return (pair,) * 4, back_finish

    def back_finish(m, rs, state):
        for d in PAIR:
            sums[d, m, :, rs, :] = state[2 + d] / jnp.maximum(nuv[d, :, rs, :], 1.0)

    def back(k, m, rs, get, state):
        x, total = list(state[:2]), list(state[2:])
        level = k.astype(F32)
        for d in PAIR:
            e, n = sol[d][k, m, :, rs, :], nuv[d, :, rs, :]
            x[d] = e + table[1, k] * jnp.where(n > level + 1.0, x[d], e * table[2, k])
            sol[d][k, m, :, rs, :] = x[d]
            total[d] = total[d] + jnp.where(n > level, x[d], 0.0)
        return (*x, *total)

    for_strips(back, back_init, reverse=True)

    def tracer_init(m, rs):
        return (pair,) * 2, lambda *a: None

    def tracers(k, m, rs, get, state):
        level = k.astype(F32)
        u, v, vs = 0.5 * get(U, k, slice(0, 3)), 0.5 * get(V, k, OWN), 0.5 * get(V, k, OWN, -1)
        out = []
        for f, e in zip((T, S), state):
            t = get(f, k, slice(0, 3))
            fx = u * (t + jnp.concatenate([east_block(t), t[:1]], axis=0))
            t = t[OWN]
            b = t - fx[OWN] + west_block(fx) - v * (t + get(f, k, OWN, 1)) + vs * (t + get(f, k, OWN, -1))
            b = jnp.where(kmt[:, rs, :] > level, b, 0.0)
            out.append((b + DIFF_NUMBER * e) * table[3, k])
            sol[f][k, m, :, rs, :] = out[-1]
        return tuple(out)

    @pl.when(has_n)
    def _():
        to_s_later.wait_recv()

    @pl.when(has_s)
    def _():
        to_n_later.wait_recv()

    lax.fori_loop(0, L // 4, unpack_rows_later, 0)
    for_strips(tracers, tracer_init)
    acc[...] = jnp.zeros(acc.shape, F32)

    collect(lambda m: fstage.at[m], lambda m: fstage_w.at[m], FX, 2, frow_sem, fe_sem, fw_sem, fpk_e, fpk_w)

    def subcycles(first, last, tiles):
        base = PAD + chip * (8 * (12 - tiles))

        def body(n, carry):
            def rows_of(t):
                return aligned(base + 8 * t)

            def eta_tile(t):
                rs = rows_of(t)
                u, v = frame[TX, :, rs, :], frame[TY, :, rs, :]
                div = (u - west(u)) + (v - frame[TY, :, pl.ds(base + 8 * t - 1, 8), :])
                eta = frame[ETA, :, rs, :] - coef[0, :, rs, :] * div
                frame[ETA, :, rs, :] = eta
                return u, v, WAVE_COURANT * eta

            last_row = iota((3, 8, 128), 1) == 7
            following = eta_tile(0)
            for t in range(tiles):
                u, v, e = following
                if t + 1 < tiles:
                    following = eta_tile(t + 1)
                else:
                    following = (None, None, WAVE_COURANT * frame[ETA, :, rows_of(tiles), :])
                e_n = jnp.where(last_row, pltpu.roll(following[2], 7, 1), pltpu.roll(e, 7, 1))
                rs = rows_of(t)
                frame[TX, :, rs, :] = u + frame[FX, :, rs, :] - coef[1, :, rs, :] * (east(e) - e)
                frame[TY, :, rs, :] = v + frame[FY, :, rs, :] - coef[2, :, rs, :] * (e_n - e)
            chip_rows = aligned(PAD + 2 * ROWS * chip, 2 * ROWS)
            acc[...] += stage[1, KMT, n // ROWS, pl.ds(lax.rem(n, ROWS), 1), :] * frame[pl.ds(0, 3), OWN, chip_rows, :]
            return carry

        lax.fori_loop(first, last, body, 0)

    def tiles_at(n):
        return min(-(-(2 * ROWS + sub_count - n) // 16) * 2, 12)

    n = 0
    while n < sub_count:
        last = n
        while last < sub_count and tiles_at(last) == tiles_at(n):
            last += 1
        subcycles(n, last, tiles_at(n))
        n = last

    mine = aligned(ROWS * core, ROWS)
    theirs = aligned(ROWS * (1 - core), ROWS)
    result[...] = acc[:, :, theirs, :]
    swap = send(result, result_in, 30, swap_sem, row + 1 - 2 * core, col)
    swap.start()
    swap.wait_recv()
    for m in PAIR:
        whole = jnp.where(core == m, acc[:, :, mine, :], result_in[...])
        for lt in PAIR:
            ls = pl.ds(LANES * lt, LANES)
            eta_out[m, :, ls] = whole[ETA, lt]
            tx_out[m, :, ls] = whole[TX, lt]
            ty_out[m, :, ls] = whole[TY, lt]
            for d, out in enumerate((qu_out, qv_out)):
                depth = coef[1 + d, lt, own_rows, :]
                out[m, :, ls] = whole[TX + d, lt] / jnp.where(depth > 0.0, depth, 1.0) - sums[d, m, lt]
                nuv_out[d, :, ls] = nuv[d, lt]

    to_w.wait_send()
    to_e.wait_send()

    @pl.when(has_s)
    def _():
        to_s.wait_send()
        to_se.wait_send()
        to_s_later.wait_send()

    @pl.when(has_n)
    def _():
        to_n.wait_send()
        to_nw.wait_send()
        to_n_later.wait_send()

    for copy in sent:
        copy.wait_send()
    swap.wait_send()


def final_kernel(level_count, sol_u, sol_v, sol_t, sol_s, qu, qv, nuv, wet, eta_in, tx_in, ty_in, eta_out, tx_out, ty_out, u_out, v_out, t_out, s_out):
    ratio = sweep_constants(level_count, DIFF_NUMBER)[1]
    m = pl.program_id(0)
    rs = pl.ds(pl.multiple_of(pl.program_id(1) * 8, 8), 8)
    eta_out[...] = eta_in[...]
    tx_out[...] = tx_in[...]
    ty_out[...] = ty_in[...]
    for lt in PAIR:
        ls = pl.ds(LANES * lt, LANES)
        n_wet = wet[:, ls]
        for src, out in ((sol_t, t_out), (sol_s, s_out)):
            x = jnp.zeros(TILE, F32)
            for k in reversed(range(level_count)):
                e = src[k, m, lt, rs, :]
                x = e + ratio[k] * jnp.where(n_wet > k + 1, x, e * (1.0 / (1.0 - ratio[k])))
                out[k, 0, :, ls] = jnp.where(n_wet > k, x, 0.0)
        for d, (src, q, out) in enumerate(((sol_u, qu, u_out), (sol_v, qv, v_out))):
            n, mean = nuv[d, :, ls], q[0, :, ls]
            for k in range(level_count):
                out[k, 0, :, ls] = jnp.where(n > float(k), src[k, m, lt, rs, :] + mean, 0.0)


def solution(mesh):
    col_count = mesh.shape["col"]

    def local_step(vel_x, vel_y, pot_temp, salinity, surf_eta, trans_x, trans_y, col_depth, wet_levels, avg_weights):
        L = vel_x.shape[0]
        N = avg_weights.shape[0]
        hbm_spec = pl.BlockSpec(memory_space=pltpu.HBM)
        vmem_spec = pl.BlockSpec(memory_space=pltpu.VMEM)
        cube = jax.ShapeDtypeStruct(vel_x.shape, F32)
        flat = jax.ShapeDtypeStruct(surf_eta.shape, F32)
        vm = lambda *shape: pltpu.VMEM(shape, F32)
        dma = lambda n: pltpu.SemaphoreType.DMA((n,))
        stage = pl.pallas_call(
            functools.partial(stage_kernel, N),
            out_shape=jax.ShapeDtypeStruct((M, 6, M, ROWS, LANES), F32),
            in_specs=[vmem_spec] * 5 + [pl.BlockSpec(memory_space=pltpu.SMEM)],
            out_specs=vmem_spec,
            name="ocean_stage",
        )(surf_eta, trans_x, trans_y, col_depth, wet_levels, avg_weights)
        *sol, qu, qv, nuv, eta_o, tx_o, ty_o = pl.pallas_call(
            functools.partial(step_kernel, col_count, L, N),
            out_shape=[jax.ShapeDtypeStruct((L, M, M, ROWS, LANES), F32)] * 4 + [flat] * 6,
            in_specs=[hbm_spec] * 4 + [vmem_spec],
            out_specs=[vmem_spec] * 10,
            scratch_shapes=[
                vm(4, L, M, RING, XR, LANES), *[vm(4, M, 8, LANES)] * 4, vm(5, M, M * L + 8, LANES), vm(4, M, M * L, LANES), vm(5, M, M * L + 8, LANES), vm(4, M, M * L, LANES),
                *[vm(M, 8, LANES)] * 2, vm(M, ROWS + 8, LANES), vm(M, M, ROWS, LANES), vm(M, M, M, ROWS, LANES),
                *[vm(4, ROWS, LANES)] * M,
                vm(M, M, M, ROWS, LANES), *[vm(M, ROWS, LANES)] * M, *[vm(4, ROWS, LANES)] * M,
                vm(6, RING, FRAME, LANES), vm(RING, RING, FRAME, LANES), vm(RING, M, M * ROWS, LANES), *[vm(RING, M, ROWS, LANES)] * M,
                pltpu.SMEM((4, L), F32), dma(8), dma(31), dma(8), *[dma(4)] * 6, pltpu.SemaphoreType.DMA],
            compiler_params=pltpu.CompilerParams(collective_id=0, has_side_effects=True, vmem_limit_bytes=STEP_VMEM),
            name="ocean_step",
        )(vel_x, vel_y, pot_temp, salinity, stage)
        cube_spec = pl.BlockSpec((L, 1, 8, 256), lambda m, i: (0, m, i, 0))
        flat_spec = pl.BlockSpec((1, 8, 256), lambda m, i: (m, i, 0))
        outs = pl.pallas_call(
            functools.partial(final_kernel, L),
            grid=(2, 3),
            out_shape=[flat] * 3 + [cube] * 4,
            in_specs=[vmem_spec] * 4 + [flat_spec] * 2
            + [pl.BlockSpec((2, 8, 256), lambda m, i: (0, i, 0)), pl.BlockSpec((8, 256), lambda m, i: (i, 0))] + [flat_spec] * 3,
            out_specs=[flat_spec] * 3 + [cube_spec] * 4,
            name="ocean_final",
            compiler_params=pltpu.CompilerParams(vmem_limit_bytes=FINAL_VMEM),
        )(*sol, qu, qv, nuv, wet_levels, eta_o, tx_o, ty_o)
        return tuple(outs)

    spec_3d = P(None, None, "row", "col")
    spec_2d = P(None, "row", "col")
    spec_map = P("row", "col")
    return jax.shard_map(local_step, mesh=mesh, in_specs=(spec_3d,) * 4 + (spec_2d,) * 3 + (spec_map,) * 2 + (P(),),
                         out_specs=(spec_2d,) * 3 + (spec_3d,) * 4, check_vma=False)
```

time: 51.5 us -> 46.3 us (0.90)
  local copies, waits for them, and re-layouts: 5.2 us -> 0.96 us
  Pallas kernels: 45.1 us -> 44.4 us
    unnamed x14 -> x4, local copies, waits for them, and re-layouts: 5.2 us -> 0.96 us
    pallas_call x1, Pallas kernels: 41.1 us -> 38.8 us  [local_step(): pl.pallas_call(functools.partial(step_kernel, col_count, L, N), out_shape...]
    pallas_call x0 -> x1, Pallas kernels: none -> 1.7 us  [local_step(): pl.pallas_call(functools.partial(stage_kernel, N), out_shape=jax.ShapeDty...]
where the time goes in v3:
time: 46.3 us; the launch traced here: 46.1 us
  Pallas kernels  44.4 us (96%)
  local copies, waits for them, and re-layouts  0.96 us (2%)
  between operations  0.65 us (1%)
    pallas_call x1, Pallas kernels, local_step(): pl.pallas_call(functools.partial(step_kernel, col_count, L, N), out_shape...  38.8 us
    pallas_call x1, Pallas kernels, local_step(): pl.pallas_call(functools.partial(final_kernel, L), grid=(2, 3), out_shape...  3.96 us
    pallas_call x1, Pallas kernels, local_step(): pl.pallas_call(functools.partial(stage_kernel, N), out_shape=jax.ShapeDty...  1.7 us
    unnamed x4, local copies, waits for them, and re-layouts  0.96 us

profile of v3, /device:TPU:0, one launch (start us, length us, event | category | flops | bytes accessed | tf_op | source)
XLA Modules:
  0.0 46.1 jit_solution(17527698244708276384)
XLA Ops:
  0.6 1.7 %ocean_stage.1.stage = f32[2,6,2,24,128]{4,3,2,1,0:T(8,128)} custom-call(f32[2,24,256]{2,1,0:T(8,128)} %eta.1, f32[2,24,256]{2,1,0:T(8,128)} %tx.1, f32[2,24,256]{2,1,0:T(8,128)} %ty.1, f32[24,256]{1,0:T(8,128)} %depth.1, s32[24,256]{1,0:T(8,128)} %wet.1, f32[30]{0:T(128)} %weights.1), custom_call_target="tpu_custom_call" | custom-call | tf_op jit(solution)/shard_map/ocean_stage/pallas_call | solution.py:599
  2.3 0.0 copy-start
  2.3 1.0 %copy-done = f32[2,6,2,24,128]{4,3,2,1,0:T(8,128)S(1)} copy-done((f32[2,6,2,24,128]{4,3,2,1,0:T(8,128)S(1)}, f32[2,6,2,24,128]{4,3,2,1,0:T(8,128)}, u32[]{:S(2)}) %copy-start) | copy-done | bytes 294936
  3.3 0.0 copy-start.1
  3.3 38.8 %ocean_step.1 = (f32[36,2,2,24,128]{4,3,2,1,0:T(8,128)S(1)}, f32[36,2,2,24,128]{4,3,2,1,0:T(8,128)S(1)}, f32[36,2,2,24,128]{4,3,2,1,0:T(8,128)S(1)}, f32[36,2,2,...) custom-call(f32[36,2,24,256]{3,2,1,0:T(8,128)} %u_hbm.1, ...), custom_call_target="tpu_custom_call" | custom-call | tf_op jit(solution)/shard_map/ocean_step/pallas_call | solution.py:606
  42.1 0.0 copy-done.1
  42.1 4.0 %ocean_final.1 = (f32[2,24,256]{2,1,0:T(8,128)}, f32[2,24,256]{2,1,0:T(8,128)}, f32[2,24,256]{2,1,0:T(8,128)}, f32[36,2,24,256]{3,2,1,0:T(8,128)}, f32[36,2,24,2...) custom-call(f32[36,2,2,24,128]{4,3,2,1,0:T(8,128)S(1)} %get-tuple-element.17.sol_u, ...), custom_call_target="tpu_custom_call" | custom-call | tf_op jit(solution)/shard_map/ocean_final/pallas_call | solution.py:623
Async XLA Ops:
  2.3 1.0 %copy-start = (f32[2,6,2,24,128]{4,3,2,1,0:T(8,128)S(1)}, f32[2,6,2,24,128]{4,3,2,1,0:T(8,128)}, u32[]{:S(2)}) copy-start(f32[2,6,2,24,128]{4,3,2,1,0:T(8,128)} %ocean_stage.1.stage) | copy-start | bytes 884740
  3.3 38.8 %copy-start.1 = (s32[24,256]{1,0:T(8,128)S(1)}, s32[24,256]{1,0:T(8,128)}, u32[]{:S(2)}) copy-start(s32[24,256]{1,0:T(8,128)} %wet.1) | copy-start | bytes 73732

commit v4 on v3

--- a/solution.py
+++ b/solution.py
@@ -19,7 +19,9 @@
 ROWS = 24
 PAD = 8
 XR = ROWS + 2 * PAD
-EDGE_BLOCK = 4
+EDGE_BLOCK = 12
+TRACER_BLOCK = 12
+SUB_BLOCK = 3
 LEVEL_BLOCK = 12
 LANES = 128
 SUB = 8
@@ -28,7 +30,10 @@
 RING = 3
 M = 2
 STEP_VMEM, FINAL_VMEM = 46 << 20, 8 << 20
-FRAME = 4 * ROWS + 2 * PAD
+TILES = 10
+SHIFT = 16
+FPAD = SHIFT + PAD
+FRAME = 4 * ROWS + 2 * FPAD
 HALO = 32
 
 
@@ -170,47 +175,49 @@
         rcv_n[...] = jnp.zeros(rcv_n.shape, F32)
         rcv_nw[...] = jnp.zeros(rcv_nw.shape, F32)
 
-    frame[:, :, pl.ds(0, PAD), :] = jnp.zeros((6, 3, PAD, 128), F32)
-    frame[:, :, pl.ds(PAD + 4 * ROWS, PAD), :] = jnp.zeros((6, 3, PAD, 128), F32)
-
-    for copy in loads:
-        copy.wait()
+    outside = jnp.zeros((6, RING, PAD, LANES), F32)
+
+    @pl.when(chip == 0)
+    def _():
+        frame[:, :, pl.ds(FPAD - PAD, PAD), :] = outside
+
+    @pl.when(chip == 1)
+    def _():
+        frame[:, :, pl.ds(FPAD + SUB * TILES, PAD), :] = outside
+
 
     lane42 = lanes(4, 2)
-
-    def pack(g, carry):
-        west_pack, east_pack = carry
-        for k, i in [(EDGE_BLOCK * g + j, i) for j in range(EDGE_BLOCK) for i in STRIPS]:
-            slot = L * i + k
-            rs = pl.ds(PAD + SUB * i, SUB)
-            west_pack = jnp.where(lane42 == slot, turn(cube[:, k, :, 0, rs, :], slot), west_pack)
-            east_pack = jnp.where(lane42 == slot, turn(cube[:, k, :, 1, rs, :], slot + 1), east_pack)
-        return west_pack, east_pack
-
-    empty = jnp.zeros((4, M, SUB, LANES), F32)
-    west_pack, east_pack = lax.fori_loop(0, L // EDGE_BLOCK, pack, (empty, empty))
-    col_w[...] = west_pack
-    col_e[...] = east_pack
+    lane2 = lanes(M)
+    empty = jnp.zeros((M, SUB, LANES), F32)
+    for f in QUAD:
+        for copy in loads[2 * f:2 * f + 2]:
+            copy.wait()
+
+        def pack(g, carry):
+            west_pack, east_pack = carry
+            for k, i in [(EDGE_BLOCK * g + j, i) for j in range(EDGE_BLOCK) for i in STRIPS]:
+                slot = L * i + k
+                rs = pl.ds(PAD + SUB * i, SUB)
+                west_pack = jnp.where(lane2 == slot, turn(cube[f, k, :, 0, rs, :], slot), west_pack)
+                east_pack = jnp.where(lane2 == slot, turn(cube[f, k, :, 1, rs, :], slot + 1), east_pack)
+            for q in range(M * EDGE_BLOCK // SUB):
+                rows = aligned(M * EDGE_BLOCK * g + SUB * q)
+                low = high = empty
+                for j in OCTET:
+                    k, m = EDGE_BLOCK * g + (SUB * q + j) // M, j % M
+                    low = jnp.where(sub2 == j, cube[f, k, m, OWN, pl.ds(PAD - j, SUB), :], low)
+                    high = jnp.where(sub2 == j, cube[f, k, m, OWN, pl.ds(PAD + ROWS - 1 - j, SUB), :], high)
+                row_n[f, :, rows, :] = high
+                row_s[f if f < T else f + 1, :, rows, :] = low
+                if f == S:
+                    row_s[T, :, rows, :] = row_s[T + 1, :, rows, :] - (HALINE_CON / THERM_EXP) * low
+            return west_pack, east_pack
+
+        sub2 = iota((M, SUB, LANES), 1)
+        col_w[f], col_e[f] = lax.fori_loop(0, L // EDGE_BLOCK, pack, (empty, empty))
     for i in STRIPS:
         slot = 3 * L + i
         col_w[0, 0] = jnp.where(lane == slot, turn(kmt[0, pl.ds(SUB * i, SUB), :], slot), col_w[0, 0])
-
-    sub42 = iota((4, M, SUB, LANES), 2)
-
-    def pack_rows(g, carry):
-        low = high = empty
-        for j in OCTET:
-            k, m = 4 * g + j // 2, j % 2
-            low = jnp.where(sub42 == j, cube[:, k, m, OWN, pl.ds(PAD - j, 8), :], low)
-            high = jnp.where(sub42 == j, cube[:, k, m, OWN, pl.ds(PAD + ROWS - 1 - j, 8), :], high)
-        rows = aligned(SUB * g)
-        row_s[:V + 1, :, rows, :] = low[:T]
-        row_s[T, :, rows, :] = low[T] - (HALINE_CON / THERM_EXP) * low[S]
-        row_s[S:, :, rows, :] = low[T:]
-        row_n[:, :, rows, :] = high
-        return carry
-
-    lax.fori_loop(0, L // 4, pack_rows, 0)
     row_s[U, :, pl.ds(M * L, SUB), :] = kmt[:, pl.ds(0, SUB), :]
 
     pl.semaphore_wait(barrier, 11)
@@ -219,7 +226,10 @@
         return pltpu.make_async_remote_copy(
             src_ref=src, dst_ref=dst, send_sem=send_sem.at[ssem], recv_sem=rsem, device_id={"row": r, "col": c}, device_id_type=MESH)
 
-    own_rows = aligned(PAD + ROWS * row, ROWS)
+    def frame_rows(r, at_chip):
+        return aligned(FPAD + ROWS * r - SHIFT * at_chip, ROWS)
+
+    own_rows = frame_rows(row, chip)
     south, north = jnp.maximum(row - 1, 0), jnp.minimum(row + 1, 3)
     to_w = send(col_w, rcv_e, 0, edge_sem.at[0], row, west_col)
     to_e = send(col_e, rcv_w, 1, edge_sem.at[1], row, east_col)
@@ -249,7 +259,7 @@
     def exchange(block, pack_w, pack_e, first, count, base, rsem, esem, wsem, pe, pw):
         out = []
         for d, r in enumerate(peers):
-            out.append(send(block(r % 2), frame.at[pl.ds(first, count), OWN, own_rows, :], base + d, rsem.at[row], r, col))
+            out.append(send(block(r % 2), frame.at[pl.ds(first, count), OWN, frame_rows(row, r // 2), :], base + d, rsem.at[row], r, col))
         for r in QUAD:
             out.append(send(pack_w(r % 2), pe.at[row], base + 3 + 2 * r, esem.at[row], r, west_col))
             out.append(send(pack_e(r % 2), pw.at[row], base + 4 + 2 * r, wsem.at[row], r, east_col))
@@ -260,7 +270,7 @@
 
     def collect(block, pack_w, first, count, rsem, esem, wsem, pe, pw):
         for r in peers:
-            rows = aligned(PAD + ROWS * r, ROWS)
+            rows = frame_rows(r, chip)
             send(block(0), frame.at[pl.ds(first, count), OWN, rows, :], 0, rsem.at[r], r, col).wait_recv()
         for r in QUAD:
             send(pack_w(0), pe.at[r], 0, esem.at[r], r, east_col).wait_recv()
@@ -268,7 +278,7 @@
         side = lax.broadcasted_iota(jnp.int32, (ROWS, 128), 1) // HALO
         for r in QUAD:
             for j in range(count):
-                frame[first + j, 2, pl.ds(PAD + ROWS * r, ROWS), :] = jnp.where(
+                frame[first + j, 2, frame_rows(r, chip), :] = jnp.where(
                     side == 0, turn(pe[r], (128 - HALO * j) % 128), jnp.where(side == 3, turn(pw[r], (128 - HALO * j - HALO) % 128), 0.0))
 
     def stage_block(m):
@@ -307,7 +317,7 @@
     press = PRESS_SCALE / L
     pair = jnp.zeros((M, SUB, LANES), F32)
 
-    def for_strips(body, init, reverse=False, strips=(0, 1, 3)):
+    def for_strips(body, init, reverse=False, strips=(0, 1, 3), levels=LEVEL_BLOCK):
         start, step, count = strips
 
         def strip(s, carry):
@@ -322,12 +332,12 @@
             state, finish = init(m, rs)
 
             def block(b, state):
-                for j in range(LEVEL_BLOCK):
-                    k = b * LEVEL_BLOCK + j
+                for j in range(levels):
+                    k = b * levels + j
                     state = body(L - 1 - k if reverse else k, m, rs, get, state)
                 return state
 
-            finish(m, rs, lax.fori_loop(0, L // LEVEL_BLOCK, block, state))
+            finish(m, rs, lax.fori_loop(0, L // levels, block, state))
             return carry
 
         lax.fori_loop(0, M * count, strip, 0)
@@ -406,17 +416,17 @@
     collect(stage_block, stage_w, ETA, 4, row_sem, e_sem, w_sem, pk_e, pk_w)
 
     def coefficients(i, carry):
-        rs = aligned(PAD + 8 * i)
+        rs = aligned(FPAD + SUB * i)
         depth = frame[DEPTH, :, rs, :]
         depth_e = east(depth)
-        depth_n = frame[DEPTH, :, pl.ds(PAD + 8 * i + 1, 8), :]
+        depth_n = frame[DEPTH, :, pl.ds(FPAD + SUB * i + 1, SUB), :]
         wet = depth > 0.0
         coef[0, :, rs, :] = jnp.where(wet, WAVE_COURANT, 0.0)
         coef[1, :, rs, :] = jnp.where(wet & (depth_e > 0.0), 0.5 * (depth + depth_e), 0.0)
         coef[2, :, rs, :] = jnp.where(wet & (depth_n > 0.0), 0.5 * (depth + depth_n), 0.0)
         return carry
 
-    lax.fori_loop(0, 12, coefficients, 0)
+    lax.fori_loop(0, TILES, coefficients, 0)
 
     for d in PAIR:
         scale = coef[1 + d, OWN, own_rows, :] / (jnp.maximum(nuv[d], 1.0) * float(sub_count))
@@ -475,54 +485,47 @@
         to_n_later.wait_recv()
 
     lax.fori_loop(0, L // 4, unpack_rows_later, 0)
-    for_strips(tracers, tracer_init)
+    for_strips(tracers, tracer_init, levels=TRACER_BLOCK)
     acc[...] = jnp.zeros(acc.shape, F32)
 
     collect(lambda m: fstage.at[m], lambda m: fstage_w.at[m], FX, 2, frow_sem, fe_sem, fw_sem, fpk_e, fpk_w)
 
-    def subcycles(first, last, tiles):
-        base = PAD + chip * (8 * (12 - tiles))
-
-        def body(n, carry):
-            def rows_of(t):
-                return aligned(base + 8 * t)
-
-            def eta_tile(t):
-                rs = rows_of(t)
-                u, v = frame[TX, :, rs, :], frame[TY, :, rs, :]
-                div = (u - west(u)) + (v - frame[TY, :, pl.ds(base + 8 * t - 1, 8), :])
-                eta = frame[ETA, :, rs, :] - coef[0, :, rs, :] * div
-                frame[ETA, :, rs, :] = eta
-                return u, v, WAVE_COURANT * eta
-
-            last_row = iota((3, 8, 128), 1) == 7
-            following = eta_tile(0)
-            for t in range(tiles):
-                u, v, e = following
-                if t + 1 < tiles:
-                    following = eta_tile(t + 1)
-                else:
-                    following = (None, None, WAVE_COURANT * frame[ETA, :, rows_of(tiles), :])
-                e_n = jnp.where(last_row, pltpu.roll(following[2], 7, 1), pltpu.roll(e, 7, 1))
-                rs = rows_of(t)
-                frame[TX, :, rs, :] = u + frame[FX, :, rs, :] - coef[1, :, rs, :] * (east(e) - e)
-                frame[TY, :, rs, :] = v + frame[FY, :, rs, :] - coef[2, :, rs, :] * (e_n - e)
-            chip_rows = aligned(PAD + 2 * ROWS * chip, 2 * ROWS)
-            acc[...] += stage[1, KMT, n // ROWS, pl.ds(lax.rem(n, ROWS), 1), :] * frame[pl.ds(0, 3), OWN, chip_rows, :]
+    def subcycle(n, tiles, base):
+        def tile_rows(t):
+            return aligned(base + SUB * t)
+
+        def eta_tile(t):
+            rs = tile_rows(t)
+            u, v = frame[TX, :, rs, :], frame[TY, :, rs, :]
+            div = (u - west(u)) + (v - frame[TY, :, pl.ds(base + SUB * t - 1, SUB), :])
+            eta = frame[ETA, :, rs, :] - coef[0, :, rs, :] * div
+            frame[ETA, :, rs, :] = eta
+            return u, v, WAVE_COURANT * eta
+
+        last_row = iota((RING, SUB, LANES), 1) == SUB - 1
+        following = eta_tile(0)
+        for t in range(tiles):
+            u, v, e = following
+            if t + 1 < tiles:
+                following = eta_tile(t + 1)
+            e_n = jnp.where(last_row, pltpu.roll(following[2], SUB - 1, 1), pltpu.roll(e, SUB - 1, 1))
+            rs = tile_rows(t)
+            frame[TX, :, rs, :] = u + frame[FX, :, rs, :] - coef[1, :, rs, :] * (east(e) - e)
+            frame[TY, :, rs, :] = v + frame[FY, :, rs, :] - coef[2, :, rs, :] * (e_n - e)
+        chip_rows = aligned(FPAD + (M * ROWS - SHIFT) * chip, M * ROWS)
+        acc[...] += stage[1, KMT, n // ROWS, pl.ds(lax.rem(n, ROWS), 1), :] * frame[pl.ds(0, RING), OWN, chip_rows, :]
+
+    def subcycles(first, last, tiles, base):
+        def block(b, carry):
+            for j in range(SUB_BLOCK):
+                subcycle(SUB_BLOCK * b + j, tiles, base)
             return carry
 
-        lax.fori_loop(first, last, body, 0)
-
-    def tiles_at(n):
-        return min(-(-(2 * ROWS + sub_count - n) // 16) * 2, 12)
-
-    n = 0
-    while n < sub_count:
-        last = n
-        while last < sub_count and tiles_at(last) == tiles_at(n):
-            last += 1
-        subcycles(n, last, tiles_at(n))
-        n = last
+        lax.fori_loop(first // SUB_BLOCK, last // SUB_BLOCK, block, 0)
+
+    turning = -(-max(sub_count - SHIFT, 0) // SUB_BLOCK) * SUB_BLOCK
+    subcycles(0, turning, TILES, FPAD)
+    subcycles(turning, sub_count, TILES - SHIFT // SUB, FPAD + SHIFT * chip)
 
     mine = aligned(ROWS * core, ROWS)
     theirs = aligned(ROWS * (1 - core), ROWS)

time: 46.3 us -> 43.3 us (0.935)
  Pallas kernels: 44.4 us -> 41.4 us
    pallas_call x1, Pallas kernels: 38.8 us -> 35.8 us  [local_step(): pl.pallas_call(functools.partial(step_kernel, col_count, L, N), out_shape...]
where the time goes in v4:
time: 43.3 us; the launch traced here: 43 us
  Pallas kernels  41.4 us (96%)
  local copies, waits for them, and re-layouts  0.96 us (2%)
  between operations  0.65 us (2%)
    pallas_call x1, Pallas kernels, local_step(): pl.pallas_call(functools.partial(step_kernel, col_count, L, N), out_shape...  35.8 us
    pallas_call x1, Pallas kernels, local_step(): pl.pallas_call(functools.partial(final_kernel, L), grid=(2, 3), out_shape...  3.96 us
    pallas_call x1, Pallas kernels, local_step(): pl.pallas_call(functools.partial(stage_kernel, N), out_shape=jax.ShapeDty...  1.7 us
    unnamed x4, local copies, waits for them, and re-layouts  0.96 us

profile of v4, /device:TPU:0, one launch (start us, length us, event | category | flops | bytes accessed | tf_op | source)
XLA Modules:
  0.0 43.0 jit_solution(367937807954935232)
XLA Ops:
  0.6 1.7 %ocean_stage.1.stage = f32[2,6,2,24,128]{4,3,2,1,0:T(8,128)} custom-call(f32[2,24,256]{2,1,0:T(8,128)} %eta.1, f32[2,24,256]{2,1,0:T(8,128)} %tx.1, f32[2,24,256]{2,1,0:T(8,128)} %ty.1, f32[24,256]{1,0:T(8,128)} %depth.1, s32[24,256]{1,0:T(8,128)} %wet.1, f32[30]{0:T(128)} %weights.1), custom_call_target="tpu_custom_call" | custom-call | tf_op jit(solution)/shard_map/ocean_stage/pallas_call | solution.py:602
  2.3 0.0 copy-start
  2.3 1.0 %copy-done = f32[2,6,2,24,128]{4,3,2,1,0:T(8,128)S(1)} copy-done((f32[2,6,2,24,128]{4,3,2,1,0:T(8,128)S(1)}, f32[2,6,2,24,128]{4,3,2,1,0:T(8,128)}, u32[]{:S(2)}) %copy-start) | copy-done | bytes 294936
  3.3 0.0 copy-start.1
  3.3 35.8 %ocean_step.1 = (f32[36,2,2,24,128]{4,3,2,1,0:T(8,128)S(1)}, f32[36,2,2,24,128]{4,3,2,1,0:T(8,128)S(1)}, f32[36,2,2,24,128]{4,3,2,1,0:T(8,128)S(1)}, f32[36,2,2,...) custom-call(f32[36,2,24,256]{3,2,1,0:T(8,128)} %u_hbm.1, ...), custom_call_target="tpu_custom_call" | custom-call | tf_op jit(solution)/shard_map/ocean_step/pallas_call | solution.py:609
  39.1 0.0 copy-done.1
  39.1 4.0 %ocean_final.1 = (f32[2,24,256]{2,1,0:T(8,128)}, f32[2,24,256]{2,1,0:T(8,128)}, f32[2,24,256]{2,1,0:T(8,128)}, f32[36,2,24,256]{3,2,1,0:T(8,128)}, f32[36,2,24,2...) custom-call(f32[36,2,2,24,128]{4,3,2,1,0:T(8,128)S(1)} %get-tuple-element.17.sol_u, ...), custom_call_target="tpu_custom_call" | custom-call | tf_op jit(solution)/shard_map/ocean_final/pallas_call | solution.py:626
Async XLA Ops:
  2.3 1.0 %copy-start = (f32[2,6,2,24,128]{4,3,2,1,0:T(8,128)S(1)}, f32[2,6,2,24,128]{4,3,2,1,0:T(8,128)}, u32[]{:S(2)}) copy-start(f32[2,6,2,24,128]{4,3,2,1,0:T(8,128)} %ocean_stage.1.stage) | copy-start | bytes 884740
  3.3 35.8 %copy-start.1 = (s32[24,256]{1,0:T(8,128)S(1)}, s32[24,256]{1,0:T(8,128)}, u32[]{:S(2)}) copy-start(s32[24,256]{1,0:T(8,128)} %wet.1) | copy-start | bytes 73732

commit v5 on v4

--- a/solution.py
+++ b/solution.py
@@ -29,7 +29,6 @@
 PAIR, STRIPS, QUAD, OCTET = range(2), range(3), range(4), range(SUB)
 RING = 3
 M = 2
-STEP_VMEM, FINAL_VMEM = 46 << 20, 8 << 20
 TILES = 10
 SHIFT = 16
 FPAD = SHIFT + PAD
@@ -94,7 +93,7 @@
             put(m, rs, pack_w, pack_e)
 
 
-def stage_kernel(sub_count, eta, tx, ty, depth, wet_in, weights, stage):
+def stage_planes(sub_count, eta, tx, ty, depth, wet_in, weights, stage):
     for lt in PAIR:
         ls = pl.ds(LANES * lt, LANES)
         wet = wet_in[:, ls].astype(F32)
@@ -116,13 +115,13 @@
 
 def step_kernel(
     col_count, level_count, sub_count,
-    u_hbm, v_hbm, t_hbm, s_hbm, stage,
-    sol_u, sol_v, sol_t, sol_s, qu_out, qv_out, nuv_out, eta_out, tx_out, ty_out,
-    cube,
+    u_hbm, v_hbm, t_hbm, s_hbm, eta_hbm, tx_hbm, ty_hbm, depth_hbm, wet_hbm, weights,
+    xu_hbm, xv_hbm, ct_hbm, cs_hbm, qu_out, qv_out, nuv_out, eta_out, tx_out, ty_out,
+    cube, sol_u, sol_v, sol_t, sol_s, eta_in, tx_in, ty_in, depth_in, wet_in, stage,
     col_w, col_e, rcv_e, rcv_w, row_s, row_n, rcv_n, rcv_s, rcv_se, rcv_nw,
     kmt, nuv, sums, pk_e, pk_w, fstage, fstage_w, fstage_e, fpk_e, fpk_w,
     frame, coef, acc, result, result_in,
-    table, load_sem, send_sem, edge_sem, row_sem, e_sem, w_sem, frow_sem, fe_sem, fw_sem, swap_sem,
+    table, load_sem, small_sem, store_sem, send_sem, edge_sem, row_sem, e_sem, w_sem, frow_sem, fe_sem, fw_sem, swap_sem,
 ):
     L = level_count
     U, V, T, S = range(4)
@@ -161,7 +160,10 @@
         for k in range(L):
             table[n, k] = line[k]
 
-    kmt[:, pl.ds(0, ROWS), :] = stage[0, KMT]
+    smalls = []
+    for n, (src, dst) in enumerate(((wet_hbm, wet_in), (eta_hbm, eta_in), (tx_hbm, tx_in), (ty_hbm, ty_in), (depth_hbm, depth_in))):
+        smalls.append(pltpu.make_async_copy(src, dst, small_sem.at[n]))
+        smalls[-1].start()
 
     has_s, has_n = row > 0, row < 3
 
@@ -215,6 +217,9 @@
 
         sub2 = iota((M, SUB, LANES), 1)
         col_w[f], col_e[f] = lax.fori_loop(0, L // EDGE_BLOCK, pack, (empty, empty))
+    smalls[0].wait()
+    for lt in PAIR:
+        kmt[lt, pl.ds(0, ROWS), :] = wet_in[:, pl.ds(LANES * lt, LANES)].astype(F32)
     for i in STRIPS:
         slot = 3 * L + i
         col_w[0, 0] = jnp.where(lane == slot, turn(kmt[0, pl.ds(SUB * i, SUB), :], slot), col_w[0, 0])
@@ -289,6 +294,10 @@
 
     def stage_e(m):
         return stage.at[m, PACK, 1]
+
+    for copy in smalls[1:]:
+        copy.wait()
+    stage_planes(sub_count, eta_in, tx_in, ty_in, depth_in, wet_in, weights, stage)
 
     to_w.wait_recv()
     to_e.wait_recv()
@@ -458,6 +467,16 @@
         return (*x, *total)
 
     for_strips(back, back_init, reverse=True)
+    stores = []
+
+    def store(f, dst):
+        for lt in PAIR:
+            stores.append(pltpu.make_async_copy(
+                sol[f].at[:, :, lt], dst.at[:, :, :, pl.ds(LANES * lt, LANES)], store_sem.at[2 * f + lt]))
+            stores[-1].start()
+
+    store(U, xu_hbm)
+    store(V, xv_hbm)
 
     def tracer_init(m, rs):
         return (pair,) * 2, lambda *a: None
@@ -486,6 +505,8 @@
 
     lax.fori_loop(0, L // 4, unpack_rows_later, 0)
     for_strips(tracers, tracer_init, levels=TRACER_BLOCK)
+    store(T, ct_hbm)
+    store(S, cs_hbm)
     acc[...] = jnp.zeros(acc.shape, F32)
 
     collect(lambda m: fstage.at[m], lambda m: fstage_w.at[m], FX, 2, frow_sem, fe_sem, fw_sem, fpk_e, fpk_w)
@@ -545,6 +566,8 @@
                 out[m, :, ls] = whole[TX + d, lt] / jnp.where(depth > 0.0, depth, 1.0) - sums[d, m, lt]
                 nuv_out[d, :, ls] = nuv[d, lt]
 
+    for copy in stores:
+        copy.wait()
     to_w.wait_send()
     to_e.wait_send()
 
@@ -565,26 +588,70 @@
     swap.wait_send()
 
 
-def final_kernel(level_count, sol_u, sol_v, sol_t, sol_s, qu, qv, nuv, wet, eta_in, tx_in, ty_in, eta_out, tx_out, ty_out, u_out, v_out, t_out, s_out):
+def final_kernel(level_count, xu, xv, ct, cs, qu, qv, nuv, wet, eta_in, tx_in, ty_in,
+                 eta_out, tx_out, ty_out, u_out, v_out, t_out, s_out,
+                 cubes, planes, wet_v, cube_in, cube_out, plane_in, plane_out):
     ratio = sweep_constants(level_count, DIFF_NUMBER)[1]
-    m = pl.program_id(0)
-    rs = pl.ds(pl.multiple_of(pl.program_id(1) * 8, 8), 8)
-    eta_out[...] = eta_in[...]
-    tx_out[...] = tx_in[...]
-    ty_out[...] = ty_in[...]
-    for lt in PAIR:
-        ls = pl.ds(LANES * lt, LANES)
-        n_wet = wet[:, ls]
-        for src, out in ((sol_t, t_out), (sol_s, s_out)):
-            x = jnp.zeros(TILE, F32)
-            for k in reversed(range(level_count)):
-                e = src[k, m, lt, rs, :]
-                x = e + ratio[k] * jnp.where(n_wet > k + 1, x, e * (1.0 / (1.0 - ratio[k])))
-                out[k, 0, :, ls] = jnp.where(n_wet > k, x, 0.0)
-        for d, (src, q, out) in enumerate(((sol_u, qu, u_out), (sol_v, qv, v_out))):
-            n, mean = nuv[d, :, ls], q[0, :, ls]
-            for k in range(level_count):
-                out[k, 0, :, ls] = jnp.where(n > float(k), src[k, m, lt, rs, :] + mean, 0.0)
+    strips = M * len(STRIPS)
+
+    def block(array, s):
+        m = s // 3
+        return array.at[:, m, pl.ds(pl.multiple_of(SUB * (s - 3 * m), SUB), SUB), :]
+
+    def reads(s):
+        return [pltpu.make_async_copy(block(src, s), cubes.at[f, s], cube_in.at[f, s]) for f, src in enumerate((ct, cs, xu, xv))]
+
+    def writes(s):
+        return [pltpu.make_async_copy(cubes.at[f, s], block(dst, s), cube_out.at[f, s]) for f, dst in enumerate((t_out, s_out, u_out, v_out))]
+
+    small = [pltpu.make_async_copy(src, planes.at[n], plane_in.at[n]) for n, src in enumerate((qu, qv, nuv, eta_in, tx_in, ty_in))]
+    small.append(pltpu.make_async_copy(wet, wet_v, plane_in.at[6]))
+    passed = [pltpu.make_async_copy(planes.at[3 + n], dst, plane_out.at[n]) for n, dst in enumerate((eta_out, tx_out, ty_out))]
+
+    def start(s, carry):
+        for copy in reads(s):
+            copy.start()
+        return carry
+
+    for copy in reads(0) + small:
+        copy.start()
+    lax.fori_loop(1, strips, start, 0)
+    for copy in small:
+        copy.wait()
+    for copy in passed:
+        copy.start()
+
+    def strip(s, carry):
+        m = s // 3
+        rs = pl.ds(pl.multiple_of(SUB * (s - 3 * m), SUB), SUB)
+        done = writes(s)
+        for f, copy in enumerate(reads(s)):
+            copy.wait()
+            for lt in PAIR:
+                ls = pl.ds(LANES * lt, LANES)
+                if f < M:
+                    n_wet = wet_v[rs, ls]
+                    x = jnp.zeros(TILE, F32)
+                    for k in reversed(range(level_count)):
+                        e = cubes[f, s, k, :, ls]
+                        x = e + ratio[k] * jnp.where(n_wet > k + 1, x, e * (1.0 / (1.0 - ratio[k])))
+                        cubes[f, s, k, :, ls] = jnp.where(n_wet > k, x, 0.0)
+                else:
+                    n, mean = planes[2, f - M, rs, ls], planes[f - M, m, rs, ls]
+                    for k in range(level_count):
+                        cubes[f, s, k, :, ls] = jnp.where(n > float(k), cubes[f, s, k, :, ls] + mean, 0.0)
+            done[f].start()
+        return carry
+
+    def finish(s, carry):
+        for copy in writes(s):
+            copy.wait()
+        return carry
+
+    lax.fori_loop(0, strips, strip, 0)
+    lax.fori_loop(0, strips, finish, 0)
+    for copy in passed:
+        copy.wait()
 
 
 def solution(mesh):
@@ -599,40 +666,33 @@
         flat = jax.ShapeDtypeStruct(surf_eta.shape, F32)
         vm = lambda *shape: pltpu.VMEM(shape, F32)
         dma = lambda n: pltpu.SemaphoreType.DMA((n,))
-        stage = pl.pallas_call(
-            functools.partial(stage_kernel, N),
-            out_shape=jax.ShapeDtypeStruct((M, 6, M, ROWS, LANES), F32),
-            in_specs=[vmem_spec] * 5 + [pl.BlockSpec(memory_space=pltpu.SMEM)],
-            out_specs=vmem_spec,
-            name="ocean_stage",
-        )(surf_eta, trans_x, trans_y, col_depth, wet_levels, avg_weights)
-        *sol, qu, qv, nuv, eta_o, tx_o, ty_o = pl.pallas_call(
+        outs = pl.pallas_call(
             functools.partial(step_kernel, col_count, L, N),
-            out_shape=[jax.ShapeDtypeStruct((L, M, M, ROWS, LANES), F32)] * 4 + [flat] * 6,
-            in_specs=[hbm_spec] * 4 + [vmem_spec],
-            out_specs=[vmem_spec] * 10,
+            out_shape=[cube] * 4 + [flat] * 6,
+            in_specs=[hbm_spec] * 9 + [pl.BlockSpec(memory_space=pltpu.SMEM)],
+            out_specs=[hbm_spec] * 4 + [vmem_spec] * 6,
             scratch_shapes=[
-                vm(4, L, M, RING, XR, LANES), *[vm(4, M, 8, LANES)] * 4, vm(5, M, M * L + 8, LANES), vm(4, M, M * L, LANES), vm(5, M, M * L + 8, LANES), vm(4, M, M * L, LANES),
+                vm(4, L, M, RING, XR, LANES), *[vm(L, M, M, ROWS, LANES)] * 4, *[vm(M, ROWS, 256)] * 3, vm(ROWS, 256),
+                pltpu.VMEM((ROWS, 256), jnp.int32), vm(M, 6, M, ROWS, LANES),
+*[vm(4, M, 8, LANES)] * 4, vm(5, M, M * L + 8, LANES), vm(4, M, M * L, LANES), vm(5, M, M * L + 8, LANES), vm(4, M, M * L, LANES),
                 *[vm(M, 8, LANES)] * 2, vm(M, ROWS + 8, LANES), vm(M, M, ROWS, LANES), vm(M, M, M, ROWS, LANES),
                 *[vm(4, ROWS, LANES)] * M,
                 vm(M, M, M, ROWS, LANES), *[vm(M, ROWS, LANES)] * M, *[vm(4, ROWS, LANES)] * M,
                 vm(6, RING, FRAME, LANES), vm(RING, RING, FRAME, LANES), vm(RING, M, M * ROWS, LANES), *[vm(RING, M, ROWS, LANES)] * M,
-                pltpu.SMEM((4, L), F32), dma(8), dma(31), dma(8), *[dma(4)] * 6, pltpu.SemaphoreType.DMA],
-            compiler_params=pltpu.CompilerParams(collective_id=0, has_side_effects=True, vmem_limit_bytes=STEP_VMEM),
+                pltpu.SMEM((4, L), F32), dma(8), dma(5), dma(8), dma(31), dma(8), *[dma(4)] * 6, pltpu.SemaphoreType.DMA],
+            compiler_params=pltpu.CompilerParams(collective_id=0, has_side_effects=True),
             name="ocean_step",
-        )(vel_x, vel_y, pot_temp, salinity, stage)
-        cube_spec = pl.BlockSpec((L, 1, 8, 256), lambda m, i: (0, m, i, 0))
-        flat_spec = pl.BlockSpec((1, 8, 256), lambda m, i: (m, i, 0))
+        )(vel_x, vel_y, pot_temp, salinity, surf_eta, trans_x, trans_y, col_depth, wet_levels, avg_weights)
+        strips = M * len(STRIPS)
         outs = pl.pallas_call(
             functools.partial(final_kernel, L),
-            grid=(2, 3),
             out_shape=[flat] * 3 + [cube] * 4,
-            in_specs=[vmem_spec] * 4 + [flat_spec] * 2
-            + [pl.BlockSpec((2, 8, 256), lambda m, i: (0, i, 0)), pl.BlockSpec((8, 256), lambda m, i: (i, 0))] + [flat_spec] * 3,
-            out_specs=[flat_spec] * 3 + [cube_spec] * 4,
+            in_specs=[hbm_spec] * 11,
+            out_specs=[hbm_spec] * 7,
+            scratch_shapes=[vm(4, strips, L, SUB, 256), vm(6, M, ROWS, 256), pltpu.VMEM((ROWS, 256), jnp.int32),
+                            pltpu.SemaphoreType.DMA((4, strips)), pltpu.SemaphoreType.DMA((4, strips)), dma(7), dma(3)],
             name="ocean_final",
-            compiler_params=pltpu.CompilerParams(vmem_limit_bytes=FINAL_VMEM),
-        )(*sol, qu, qv, nuv, wet_levels, eta_o, tx_o, ty_o)
+        )(*outs[:7], wet_levels, *outs[7:])
         return tuple(outs)
 
     spec_3d = P(None, None, "row", "col")

time: 43.3 us -> 44.7 us (1.032)
  Pallas kernels: 41.4 us -> 43.9 us
  local copies, waits for them, and re-layouts: 0.96 us -> 0 us
    pallas_call x1, Pallas kernels: 35.8 us -> 37.5 us  [local_step(): pl.pallas_call(functools.partial(step_kernel, col_count, L, N), out_shape...]
    unnamed x4 -> x0, local copies, waits for them, and re-layouts: 0.96 us -> none
    pallas_call x2 -> x1, Pallas kernels: 5.66 us -> 6.4 us  [local_step(): pl.pallas_call(functools.partial(final_kernel, L), out_shape=[flat] * 3 +...]
where the time goes in v5:
time: 44.7 us; the launch traced here: 44.6 us
  Pallas kernels  43.9 us (98%)
  between operations  0.64 us (1%)
    pallas_call x1, Pallas kernels, local_step(): pl.pallas_call(functools.partial(step_kernel, col_count, L, N), out_shape...  37.5 us
    pallas_call x1, Pallas kernels, local_step(): pl.pallas_call(functools.partial(final_kernel, L), out_shape=[flat] * 3 +...  6.4 us

profile of v5, /device:TPU:0, one launch (start us, length us, event | category | flops | bytes accessed | tf_op | source)
XLA Modules:
  0.0 44.6 jit_solution(8050833444583275903)
XLA Ops:
  0.6 37.5 %ocean_step.1 = (f32[36,2,24,256]{3,2,1,0:T(8,128)}, f32[36,2,24,256]{3,2,1,0:T(8,128)}, f32[36,2,24,256]{3,2,1,0:T(8,128)}, f32[36,2,24,256]{3,2,1,0:T(8,128)},...) custom-call(f32[36,2,24,256]{3,2,1,0:T(8,128)} %u_hbm.1, ...), custom_call_target="tpu_custom_call" | custom-call | tf_op jit(solution)/shard_map/ocean_step/pallas_call | solution.py:669
  38.2 6.4 %ocean_final.1 = (f32[2,24,256]{2,1,0:T(8,128)}, f32[2,24,256]{2,1,0:T(8,128)}, f32[2,24,256]{2,1,0:T(8,128)}, f32[36,2,24,256]{3,2,1,0:T(8,128)}, f32[36,2,24,2...) custom-call(f32[36,2,24,256]{3,2,1,0:T(8,128)} %get-tuple-element.17.xu, ...), custom_call_target="tpu_custom_call" | custom-call | tf_op jit(solution)/shard_map/ocean_final/pallas_call | solution.py:687

commit v6 on v4

--- a/solution.py
+++ b/solution.py
@@ -21,6 +21,7 @@
 XR = ROWS + 2 * PAD
 EDGE_BLOCK = 12
 TRACER_BLOCK = 12
+BACK_BLOCK = 6
 SUB_BLOCK = 3
 LEVEL_BLOCK = 12
 LANES = 128
@@ -29,7 +30,7 @@
 PAIR, STRIPS, QUAD, OCTET = range(2), range(3), range(4), range(SUB)
 RING = 3
 M = 2
-STEP_VMEM, FINAL_VMEM = 46 << 20, 8 << 20
+STEP_VMEM, FINAL_VMEM = 46 << 20, 9 << 20
 TILES = 10
 SHIFT = 16
 FPAD = SHIFT + PAD
@@ -317,7 +318,7 @@
     press = PRESS_SCALE / L
     pair = jnp.zeros((M, SUB, LANES), F32)
 
-    def for_strips(body, init, reverse=False, strips=(0, 1, 3), levels=LEVEL_BLOCK):
+    def for_strips(body, init, strips=(0, 1, 3), levels=LEVEL_BLOCK):
         start, step, count = strips
 
         def strip(s, carry):
@@ -334,7 +335,7 @@
             def block(b, state):
                 for j in range(levels):
                     k = b * levels + j
-                    state = body(L - 1 - k if reverse else k, m, rs, get, state)
+                    state = body(k, m, rs, get, state)
                 return state
 
             finish(m, rs, lax.fori_loop(0, L // levels, block, state))
@@ -354,15 +355,15 @@
         level = k.astype(F32)
         both = slice(0, 3)
         u, v, un, vs = get(U, k, both), get(V, k, both), get(U, k, both, 1), get(V, k, both, -1)
-        rho = HALINE_CON * get(S, k, both) - THERM_EXP * get(T, k, both)
+        rho = (press * HALINE_CON) * get(S, k, both) - (press * THERM_EXP) * get(T, k, both)
         dx = rho[OWN] - east_block(rho)
-        dy = rho[OWN] - (HALINE_CON * get(S, k, OWN, 1) - THERM_EXP * get(T, k, OWN, 1))
+        dy = rho[OWN] - ((press * HALINE_CON) * get(S, k, OWN, 1) - (press * THERM_EXP) * get(T, k, OWN, 1))
         vsum, usum = v + vs, u + un
         cx, cy = cx + dx, cy + dy
-        gu = press * (cx - 0.5 * dx) - 0.5 * (u[OWN] * (east_block(u) - west_block(u))) - 0.125 * (
+        gu = cx - 0.5 * (dx + u[OWN] * (east_block(u) - west_block(u))) - 0.125 * (
             (vsum[OWN] + east_block(vsum)) * (un[OWN] - get(U, k, OWN, -1)))
-        gv = press * (cy - 0.5 * dy) - 0.125 * ((usum[OWN] + west_block(usum)) * (east_block(v) - west_block(v))) - 0.5 * (
-            v[OWN] * (get(V, k, OWN, 1) - vs[OWN]))
+        gv = cy - 0.5 * (dy + v[OWN] * (get(V, k, OWN, 1) - vs[OWN])) - 0.125 * (
+            (usum[OWN] + west_block(usum)) * (east_block(v) - west_block(v)))
         gu = jnp.where(nuv[0, :, rs, :] > level, gu, 0.0)
         gv = jnp.where(nuv[1, :, rs, :] > level, gv, 0.0)
         inverse = table[0, k]
@@ -422,14 +423,14 @@
         depth_n = frame[DEPTH, :, pl.ds(FPAD + SUB * i + 1, SUB), :]
         wet = depth > 0.0
         coef[0, :, rs, :] = jnp.where(wet, WAVE_COURANT, 0.0)
-        coef[1, :, rs, :] = jnp.where(wet & (depth_e > 0.0), 0.5 * (depth + depth_e), 0.0)
-        coef[2, :, rs, :] = jnp.where(wet & (depth_n > 0.0), 0.5 * (depth + depth_n), 0.0)
+        coef[1, :, rs, :] = jnp.where(wet & (depth_e > 0.0), (0.5 * WAVE_COURANT) * (depth + depth_e), 0.0)
+        coef[2, :, rs, :] = jnp.where(wet & (depth_n > 0.0), (0.5 * WAVE_COURANT) * (depth + depth_n), 0.0)
         return carry
 
     lax.fori_loop(0, TILES, coefficients, 0)
 
     for d in PAIR:
-        scale = coef[1 + d, OWN, own_rows, :] / (jnp.maximum(nuv[d], 1.0) * float(sub_count))
+        scale = coef[1 + d, OWN, own_rows, :] / (jnp.maximum(nuv[d], 1.0) * (WAVE_COURANT * sub_count))
         for m in PAIR:
             fstage[m, d] = scale * sums[d, m]
 
@@ -440,41 +441,42 @@
     pack_2d(fstage, 2, put)
     sent += exchange(lambda m: fstage.at[m], lambda m: fstage_w.at[m], lambda m: fstage_e.at[m], FX, 2, 19, frow_sem, fe_sem, fw_sem, fpk_e, fpk_w)
 
-    def back_init(m, rs):
-        return (pair,) * 4, back_finish
-
-    def back_finish(m, rs, state):
+    block_zero = jnp.zeros((M, ROWS, LANES), F32)
+
+    def back(m, carry):
+        def levels_back(b, state):
+            x, total = list(state[:2]), list(state[2:])
+            for j in range(BACK_BLOCK):
+                k = L - 1 - (b * BACK_BLOCK + j)
+                level = k.astype(F32)
+                for d in PAIR:
+                    e, n = sol[d][k, m], nuv[d]
+                    x[d] = e + table[1, k] * jnp.where(n > level + 1.0, x[d], e * table[2, k])
+                    sol[d][k, m] = x[d]
+                    total[d] = total[d] + jnp.where(n > level, x[d], 0.0)
+            return (*x, *total)
+
+        state = lax.fori_loop(0, L // BACK_BLOCK, levels_back, (block_zero,) * 4)
         for d in PAIR:
-            sums[d, m, :, rs, :] = state[2 + d] / jnp.maximum(nuv[d, :, rs, :], 1.0)
-
-    def back(k, m, rs, get, state):
-        x, total = list(state[:2]), list(state[2:])
-        level = k.astype(F32)
-        for d in PAIR:
-            e, n = sol[d][k, m, :, rs, :], nuv[d, :, rs, :]
-            x[d] = e + table[1, k] * jnp.where(n > level + 1.0, x[d], e * table[2, k])
-            sol[d][k, m, :, rs, :] = x[d]
-            total[d] = total[d] + jnp.where(n > level, x[d], 0.0)
-        return (*x, *total)
-
-    for_strips(back, back_init, reverse=True)
+            sums[d, m] = state[2 + d] / jnp.maximum(nuv[d], 1.0)
+        return carry
+
+    lax.fori_loop(0, M, back, 0)
 
     def tracer_init(m, rs):
-        return (pair,) * 2, lambda *a: None
-
-    def tracers(k, m, rs, get, state):
-        level = k.astype(F32)
-        u, v, vs = 0.5 * get(U, k, slice(0, 3)), 0.5 * get(V, k, OWN), 0.5 * get(V, k, OWN, -1)
-        out = []
-        for f, e in zip((T, S), state):
-            t = get(f, k, slice(0, 3))
+        return pair, lambda *a: None
+
+    def tracer(f):
+        def body(k, m, rs, get, e):
+            t, u = get(f, k, slice(0, 3)), get(U, k, slice(0, 3))
             fx = u * (t + jnp.concatenate([east_block(t), t[:1]], axis=0))
             t = t[OWN]
-            b = t - fx[OWN] + west_block(fx) - v * (t + get(f, k, OWN, 1)) + vs * (t + get(f, k, OWN, -1))
-            b = jnp.where(kmt[:, rs, :] > level, b, 0.0)
-            out.append((b + DIFF_NUMBER * e) * table[3, k])
-            sol[f][k, m, :, rs, :] = out[-1]
-        return tuple(out)
+            gain = fx[OWN] - west_block(fx) + (get(V, k, OWN) * (t + get(f, k, OWN, 1)) - get(V, k, OWN, -1) * (t + get(f, k, OWN, -1)))
+            e = (jnp.where(kmt[:, rs, :] > k.astype(F32), t - 0.5 * gain, 0.0) + DIFF_NUMBER * e) * table[3, k]
+            sol[f][k, m, :, rs, :] = e
+            return e
+
+        return body
 
     @pl.when(has_n)
     def _():
@@ -485,7 +487,8 @@
         to_n_later.wait_recv()
 
     lax.fori_loop(0, L // 4, unpack_rows_later, 0)
-    for_strips(tracers, tracer_init, levels=TRACER_BLOCK)
+    for f in (T, S):
+        for_strips(tracer(f), tracer_init, levels=TRACER_BLOCK)
     acc[...] = jnp.zeros(acc.shape, F32)
 
     collect(lambda m: fstage.at[m], lambda m: fstage_w.at[m], FX, 2, frow_sem, fe_sem, fw_sem, fpk_e, fpk_w)
@@ -500,7 +503,7 @@
             div = (u - west(u)) + (v - frame[TY, :, pl.ds(base + SUB * t - 1, SUB), :])
             eta = frame[ETA, :, rs, :] - coef[0, :, rs, :] * div
             frame[ETA, :, rs, :] = eta
-            return u, v, WAVE_COURANT * eta
+            return u, v, eta
 
         last_row = iota((RING, SUB, LANES), 1) == SUB - 1
         following = eta_tile(0)
@@ -542,7 +545,7 @@
             ty_out[m, :, ls] = whole[TY, lt]
             for d, out in enumerate((qu_out, qv_out)):
                 depth = coef[1 + d, lt, own_rows, :]
-                out[m, :, ls] = whole[TX + d, lt] / jnp.where(depth > 0.0, depth, 1.0) - sums[d, m, lt]
+                out[m, :, ls] = whole[TX + d, lt] / jnp.where(depth > 0.0, depth / WAVE_COURANT, 1.0) - sums[d, m, lt]
                 nuv_out[d, :, ls] = nuv[d, lt]
 
     to_w.wait_send()
@@ -565,26 +568,46 @@
     swap.wait_send()
 
 
-def final_kernel(level_count, sol_u, sol_v, sol_t, sol_s, qu, qv, nuv, wet, eta_in, tx_in, ty_in, eta_out, tx_out, ty_out, u_out, v_out, t_out, s_out):
+def final_kernel(level_count, sol_u, sol_v, sol_t, sol_s, qu, qv, nuv, wet, eta_in, tx_in, ty_in,
+                 eta_out, tx_out, ty_out, u_out, v_out, t_out, s_out, cubes, cube_sem):
     ratio = sweep_constants(level_count, DIFF_NUMBER)[1]
-    m = pl.program_id(0)
-    rs = pl.ds(pl.multiple_of(pl.program_id(1) * 8, 8), 8)
+    strips = M * len(STRIPS)
     eta_out[...] = eta_in[...]
     tx_out[...] = tx_in[...]
     ty_out[...] = ty_in[...]
-    for lt in PAIR:
-        ls = pl.ds(LANES * lt, LANES)
-        n_wet = wet[:, ls]
-        for src, out in ((sol_t, t_out), (sol_s, s_out)):
-            x = jnp.zeros(TILE, F32)
-            for k in reversed(range(level_count)):
-                e = src[k, m, lt, rs, :]
-                x = e + ratio[k] * jnp.where(n_wet > k + 1, x, e * (1.0 / (1.0 - ratio[k])))
-                out[k, 0, :, ls] = jnp.where(n_wet > k, x, 0.0)
-        for d, (src, q, out) in enumerate(((sol_u, qu, u_out), (sol_v, qv, v_out))):
-            n, mean = nuv[d, :, ls], q[0, :, ls]
-            for k in range(level_count):
-                out[k, 0, :, ls] = jnp.where(n > float(k), src[k, m, lt, rs, :] + mean, 0.0)
+
+    def writes(s):
+        m = s // 3
+        rs = pl.ds(pl.multiple_of(SUB * (s - 3 * m), SUB), SUB)
+        return m, rs, [pltpu.make_async_copy(cubes.at[f, s], dst.at[:, m, rs, :], cube_sem.at[f, s])
+                       for f, dst in enumerate((t_out, s_out, u_out, v_out))]
+
+    def strip(s, carry):
+        m, rs, done = writes(s)
+        for f, src in enumerate((sol_t, sol_s, sol_u, sol_v)):
+            for lt in PAIR:
+                ls = pl.ds(LANES * lt, LANES)
+                if f < M:
+                    n_wet = wet[rs, ls]
+                    x = jnp.zeros(TILE, F32)
+                    for k in reversed(range(level_count)):
+                        e = src[k, m, lt, rs, :]
+                        x = e + ratio[k] * jnp.where(n_wet > k + 1, x, e * (1.0 / (1.0 - ratio[k])))
+                        cubes[f, s, k, :, ls] = jnp.where(n_wet > k, x, 0.0)
+                else:
+                    n, mean = nuv[f - M, rs, ls], (qu, qv)[f - M][m, rs, ls]
+                    for k in range(level_count):
+                        cubes[f, s, k, :, ls] = jnp.where(n > float(k), src[k, m, lt, rs, :] + mean, 0.0)
+            done[f].start()
+        return carry
+
+    def finish(s, carry):
+        for copy in writes(s)[-1]:
+            copy.wait()
+        return carry
+
+    lax.fori_loop(0, strips, strip, 0)
+    lax.fori_loop(0, strips, finish, 0)
 
 
 def solution(mesh):
@@ -621,15 +644,12 @@
             compiler_params=pltpu.CompilerParams(collective_id=0, has_side_effects=True, vmem_limit_bytes=STEP_VMEM),
             name="ocean_step",
         )(vel_x, vel_y, pot_temp, salinity, stage)
-        cube_spec = pl.BlockSpec((L, 1, 8, 256), lambda m, i: (0, m, i, 0))
-        flat_spec = pl.BlockSpec((1, 8, 256), lambda m, i: (m, i, 0))
         outs = pl.pallas_call(
             functools.partial(final_kernel, L),
-            grid=(2, 3),
             out_shape=[flat] * 3 + [cube] * 4,
-            in_specs=[vmem_spec] * 4 + [flat_spec] * 2
-            + [pl.BlockSpec((2, 8, 256), lambda m, i: (0, i, 0)), pl.BlockSpec((8, 256), lambda m, i: (i, 0))] + [flat_spec] * 3,
-            out_specs=[flat_spec] * 3 + [cube_spec] * 4,
+            in_specs=[vmem_spec] * 11,
+            out_specs=[vmem_spec] * 3 + [hbm_spec] * 4,
+            scratch_shapes=[vm(4, M * len(STRIPS), L, SUB, 256), pltpu.SemaphoreType.DMA((4, M * len(STRIPS)))],
             name="ocean_final",
             compiler_params=pltpu.CompilerParams(vmem_limit_bytes=FINAL_VMEM),
         )(*sol, qu, qv, nuv, wet_levels, eta_o, tx_o, ty_o)

time: 43.3 us -> 45.2 us (1.044)
  Pallas kernels: 41.4 us -> 43.4 us
    pallas_call x1, Pallas kernels: 35.8 us -> 37.8 us  [local_step(): pl.pallas_call(functools.partial(step_kernel, col_count, L, N), out_shape...]
where the time goes in v6:
time: 45.2 us; the launch traced here: 45 us
  Pallas kernels  43.4 us (96%)
  local copies, waits for them, and re-layouts  0.96 us (2%)
  between operations  0.65 us (1%)
    pallas_call x1, Pallas kernels, local_step(): pl.pallas_call(functools.partial(step_kernel, col_count, L, N), out_shape...  37.8 us
    pallas_call x1, Pallas kernels, local_step(): pl.pallas_call(functools.partial(final_kernel, L), out_shape=[flat] * 3 +...  3.89 us
    pallas_call x1, Pallas kernels, local_step(): pl.pallas_call(functools.partial(stage_kernel, N), out_shape=jax.ShapeDty...  1.7 us
    unnamed x4, local copies, waits for them, and re-layouts  0.96 us

profile of v6, /device:TPU:0, one launch (start us, length us, event | category | flops | bytes accessed | tf_op | source)
XLA Modules:
  0.0 45.0 jit_solution(4856409114879183844)
XLA Ops:
  0.6 1.7 %ocean_stage.1.stage = f32[2,6,2,24,128]{4,3,2,1,0:T(8,128)} custom-call(f32[2,24,256]{2,1,0:T(8,128)} %eta.1, f32[2,24,256]{2,1,0:T(8,128)} %tx.1, f32[2,24,256]{2,1,0:T(8,128)} %ty.1, f32[24,256]{1,0:T(8,128)} %depth.1, s32[24,256]{1,0:T(8,128)} %wet.1, f32[30]{0:T(128)} %weights.1), custom_call_target="tpu_custom_call" | custom-call | tf_op jit(solution)/shard_map/ocean_stage/pallas_call | solution.py:625
  2.3 0.0 copy-start
  2.3 1.0 %copy-done = f32[2,6,2,24,128]{4,3,2,1,0:T(8,128)S(1)} copy-done((f32[2,6,2,24,128]{4,3,2,1,0:T(8,128)S(1)}, f32[2,6,2,24,128]{4,3,2,1,0:T(8,128)}, u32[]{:S(2)}) %copy-start) | copy-done | bytes 294936
  3.3 0.0 copy-start.1
  3.3 37.8 %ocean_step.1 = (f32[36,2,2,24,128]{4,3,2,1,0:T(8,128)S(1)}, f32[36,2,2,24,128]{4,3,2,1,0:T(8,128)S(1)}, f32[36,2,2,24,128]{4,3,2,1,0:T(8,128)S(1)}, f32[36,2,2,...) custom-call(f32[36,2,24,256]{3,2,1,0:T(8,128)} %u_hbm.1, ...), custom_call_target="tpu_custom_call" | custom-call | tf_op jit(solution)/shard_map/ocean_step/pallas_call | solution.py:632
  41.1 0.0 copy-done.1
  41.1 3.9 %ocean_final.1 = (f32[2,24,256]{2,1,0:T(8,128)}, f32[2,24,256]{2,1,0:T(8,128)}, f32[2,24,256]{2,1,0:T(8,128)}, f32[36,2,24,256]{3,2,1,0:T(8,128)}, f32[36,2,24,2...) custom-call(f32[36,2,2,24,128]{4,3,2,1,0:T(8,128)S(1)} %get-tuple-element.17.sol_u, ...), custom_call_target="tpu_custom_call" | custom-call | tf_op jit(solution)/shard_map/ocean_final/pallas_call | solution.py:647
Async XLA Ops:
  2.3 1.0 %copy-start = (f32[2,6,2,24,128]{4,3,2,1,0:T(8,128)S(1)}, f32[2,6,2,24,128]{4,3,2,1,0:T(8,128)}, u32[]{:S(2)}) copy-start(f32[2,6,2,24,128]{4,3,2,1,0:T(8,128)} %ocean_stage.1.stage) | copy-start | bytes 884740
  3.3 37.8 %copy-start.1 = (s32[24,256]{1,0:T(8,128)S(1)}, s32[24,256]{1,0:T(8,128)}, u32[]{:S(2)}) copy-start(s32[24,256]{1,0:T(8,128)} %wet.1) | copy-start | bytes 73732

commit v7 on v6

--- a/solution.py
+++ b/solution.py
@@ -20,10 +20,10 @@
 PAD = 8
 XR = ROWS + 2 * PAD
 EDGE_BLOCK = 12
-TRACER_BLOCK = 12
-BACK_BLOCK = 6
+TRACER_BLOCK = 36
+BACK_BLOCK = 36
 SUB_BLOCK = 3
-LEVEL_BLOCK = 12
+LEVEL_BLOCK = 36
 LANES = 128
 SUB = 8
 TILE = (SUB, LANES)

time: 45.2 us -> 42.4 us (0.938)
  Pallas kernels: 43.4 us -> 40.5 us
    pallas_call x1, Pallas kernels: 37.8 us -> 35 us  [local_step(): pl.pallas_call(functools.partial(step_kernel, col_count, L, N), out_shape...]
where the time goes in v7:
time: 42.4 us; the launch traced here: 42.2 us
  Pallas kernels  40.5 us (96%)
  local copies, waits for them, and re-layouts  0.96 us (2%)
  between operations  0.65 us (2%)
    pallas_call x1, Pallas kernels, local_step(): pl.pallas_call(functools.partial(step_kernel, col_count, L, N), out_shape...  35 us
    pallas_call x1, Pallas kernels, local_step(): pl.pallas_call(functools.partial(final_kernel, L), out_shape=[flat] * 3 +...  3.89 us
    pallas_call x1, Pallas kernels, local_step(): pl.pallas_call(functools.partial(stage_kernel, N), out_shape=jax.ShapeDty...  1.7 us
    unnamed x4, local copies, waits for them, and re-layouts  0.96 us

profile of v7, /device:TPU:0, one launch (start us, length us, event | category | flops | bytes accessed | tf_op | source)
XLA Modules:
  0.0 42.2 jit_solution(15547547094504051567)
XLA Ops:
  0.6 1.7 %ocean_stage.1.stage = f32[2,6,2,24,128]{4,3,2,1,0:T(8,128)} custom-call(f32[2,24,256]{2,1,0:T(8,128)} %eta.1, f32[2,24,256]{2,1,0:T(8,128)} %tx.1, f32[2,24,256]{2,1,0:T(8,128)} %ty.1, f32[24,256]{1,0:T(8,128)} %depth.1, s32[24,256]{1,0:T(8,128)} %wet.1, f32[30]{0:T(128)} %weights.1), custom_call_target="tpu_custom_call" | custom-call | tf_op jit(solution)/shard_map/ocean_stage/pallas_call | solution.py:625
  2.3 0.0 copy-start
  2.3 1.0 %copy-done = f32[2,6,2,24,128]{4,3,2,1,0:T(8,128)S(1)} copy-done((f32[2,6,2,24,128]{4,3,2,1,0:T(8,128)S(1)}, f32[2,6,2,24,128]{4,3,2,1,0:T(8,128)}, u32[]{:S(2)}) %copy-start) | copy-done | bytes 294936
  3.3 0.0 copy-start.1
  3.3 35.0 %ocean_step.1 = (f32[36,2,2,24,128]{4,3,2,1,0:T(8,128)S(1)}, f32[36,2,2,24,128]{4,3,2,1,0:T(8,128)S(1)}, f32[36,2,2,24,128]{4,3,2,1,0:T(8,128)S(1)}, f32[36,2,2,...) custom-call(f32[36,2,24,256]{3,2,1,0:T(8,128)} %u_hbm.1, ...), custom_call_target="tpu_custom_call" | custom-call | tf_op jit(solution)/shard_map/ocean_step/pallas_call | solution.py:632
  38.3 0.0 copy-done.1
  38.3 3.9 %ocean_final.1 = (f32[2,24,256]{2,1,0:T(8,128)}, f32[2,24,256]{2,1,0:T(8,128)}, f32[2,24,256]{2,1,0:T(8,128)}, f32[36,2,24,256]{3,2,1,0:T(8,128)}, f32[36,2,24,2...) custom-call(f32[36,2,2,24,128]{4,3,2,1,0:T(8,128)S(1)} %get-tuple-element.17.sol_u, ...), custom_call_target="tpu_custom_call" | custom-call | tf_op jit(solution)/shard_map/ocean_final/pallas_call | solution.py:647
Async XLA Ops:
  2.3 1.0 %copy-start = (f32[2,6,2,24,128]{4,3,2,1,0:T(8,128)S(1)}, f32[2,6,2,24,128]{4,3,2,1,0:T(8,128)}, u32[]{:S(2)}) copy-start(f32[2,6,2,24,128]{4,3,2,1,0:T(8,128)} %ocean_stage.1.stage) | copy-start | bytes 884740
  3.3 35.0 %copy-start.1 = (s32[24,256]{1,0:T(8,128)S(1)}, s32[24,256]{1,0:T(8,128)}, u32[]{:S(2)}) copy-start(s32[24,256]{1,0:T(8,128)} %wet.1) | copy-start | bytes 73732

commit v8 on v7

--- a/solution.py
+++ b/solution.py
@@ -79,7 +79,9 @@
     return jnp.where(lanes(2) == 0, jnp.concatenate([x[2:], rolled[:1]], axis=0), rolled)
 
 
-ETA, TX, TY, DEPTH, PACK, KMT = range(6)
+STAGED = 6
+ROOM = 240
+ETA, TX, TY, DEPTH, PACK, KMT = range(STAGED)
 
 
 def pack_2d(stage, count, put):
@@ -95,7 +97,7 @@
             put(m, rs, pack_w, pack_e)
 
 
-def stage_kernel(sub_count, eta, tx, ty, depth, wet_in, weights, stage):
+def stage_kernel(sub_count, eta, tx, ty, depth, wet_in, weights, out, stage, sem):
     for lt in PAIR:
         ls = pl.ds(LANES * lt, LANES)
         wet = wet_in[:, ls].astype(F32)
@@ -113,17 +115,20 @@
         stage[m, PACK, 1, rs, :] = pack_e
 
     pack_2d(stage, 4, put)
+    copy = pltpu.make_async_copy(stage, out.at[:, pl.ds(0, STAGED)], sem)
+    copy.start()
+    copy.wait()
 
 
 def step_kernel(
     col_count, level_count, sub_count,
-    u_hbm, v_hbm, t_hbm, s_hbm, stage,
+    u_hbm, v_hbm, t_hbm, s_hbm, stage_hbm,
     sol_u, sol_v, sol_t, sol_s, qu_out, qv_out, nuv_out, eta_out, tx_out, ty_out,
-    cube,
+    cube, stage,
     col_w, col_e, rcv_e, rcv_w, row_s, row_n, rcv_n, rcv_s, rcv_se, rcv_nw,
     kmt, nuv, sums, pk_e, pk_w, fstage, fstage_w, fstage_e, fpk_e, fpk_w,
     frame, coef, acc, result, result_in,
-    table, load_sem, send_sem, edge_sem, row_sem, e_sem, w_sem, frow_sem, fe_sem, fw_sem, swap_sem,
+    table, load_sem, stage_sem, send_sem, edge_sem, row_sem, e_sem, w_sem, frow_sem, fe_sem, fw_sem, swap_sem,
 ):
     L = level_count
     U, V, T, S = range(4)
@@ -162,7 +167,8 @@
         for k in range(L):
             table[n, k] = line[k]
 
-    kmt[:, pl.ds(0, ROWS), :] = stage[0, KMT]
+    staged = pltpu.make_async_copy(stage_hbm.at[:, pl.ds(0, STAGED)], stage, stage_sem)
+    staged.start()
 
     has_s, has_n = row > 0, row < 3
 
@@ -216,6 +222,8 @@
 
         sub2 = iota((M, SUB, LANES), 1)
         col_w[f], col_e[f] = lax.fori_loop(0, L // EDGE_BLOCK, pack, (empty, empty))
+    staged.wait()
+    kmt[:, pl.ds(0, ROWS), :] = stage[0, KMT]
     for i in STRIPS:
         slot = 3 * L + i
         col_w[0, 0] = jnp.where(lane == slot, turn(kmt[0, pl.ds(SUB * i, SUB), :], slot), col_w[0, 0])
@@ -569,12 +577,13 @@
 
 
 def final_kernel(level_count, sol_u, sol_v, sol_t, sol_s, qu, qv, nuv, wet, eta_in, tx_in, ty_in,
-                 eta_out, tx_out, ty_out, u_out, v_out, t_out, s_out, cubes, cube_sem):
+                 eta_out, tx_out, ty_out, u_out, v_out, t_out, s_out, cubes, cube_sem, plane_sem):
     ratio = sweep_constants(level_count, DIFF_NUMBER)[1]
     strips = M * len(STRIPS)
-    eta_out[...] = eta_in[...]
-    tx_out[...] = tx_in[...]
-    ty_out[...] = ty_in[...]
+    passed = [pltpu.make_async_copy(src, dst, plane_sem.at[n])
+              for n, (src, dst) in enumerate(((eta_in, eta_out), (tx_in, tx_out), (ty_in, ty_out)))]
+    for copy in passed:
+        copy.start()
 
     def writes(s):
         m = s // 3
@@ -608,6 +617,8 @@
 
     lax.fori_loop(0, strips, strip, 0)
     lax.fori_loop(0, strips, finish, 0)
+    for copy in passed:
+        copy.wait()
 
 
 def solution(mesh):
@@ -624,23 +635,24 @@
         dma = lambda n: pltpu.SemaphoreType.DMA((n,))
         stage = pl.pallas_call(
             functools.partial(stage_kernel, N),
-            out_shape=jax.ShapeDtypeStruct((M, 6, M, ROWS, LANES), F32),
+            out_shape=jax.ShapeDtypeStruct((M, ROOM, M, ROWS, LANES), F32),
             in_specs=[vmem_spec] * 5 + [pl.BlockSpec(memory_space=pltpu.SMEM)],
-            out_specs=vmem_spec,
+            out_specs=hbm_spec,
+            scratch_shapes=[vm(M, STAGED, M, ROWS, LANES), pltpu.SemaphoreType.DMA],
             name="ocean_stage",
         )(surf_eta, trans_x, trans_y, col_depth, wet_levels, avg_weights)
         *sol, qu, qv, nuv, eta_o, tx_o, ty_o = pl.pallas_call(
             functools.partial(step_kernel, col_count, L, N),
             out_shape=[jax.ShapeDtypeStruct((L, M, M, ROWS, LANES), F32)] * 4 + [flat] * 6,
-            in_specs=[hbm_spec] * 4 + [vmem_spec],
+            in_specs=[hbm_spec] * 5,
             out_specs=[vmem_spec] * 10,
             scratch_shapes=[
-                vm(4, L, M, RING, XR, LANES), *[vm(4, M, 8, LANES)] * 4, vm(5, M, M * L + 8, LANES), vm(4, M, M * L, LANES), vm(5, M, M * L + 8, LANES), vm(4, M, M * L, LANES),
+                vm(4, L, M, RING, XR, LANES), vm(M, STAGED, M, ROWS, LANES), *[vm(4, M, 8, LANES)] * 4, vm(5, M, M * L + 8, LANES), vm(4, M, M * L, LANES), vm(5, M, M * L + 8, LANES), vm(4, M, M * L, LANES),
                 *[vm(M, 8, LANES)] * 2, vm(M, ROWS + 8, LANES), vm(M, M, ROWS, LANES), vm(M, M, M, ROWS, LANES),
                 *[vm(4, ROWS, LANES)] * M,
                 vm(M, M, M, ROWS, LANES), *[vm(M, ROWS, LANES)] * M, *[vm(4, ROWS, LANES)] * M,
                 vm(6, RING, FRAME, LANES), vm(RING, RING, FRAME, LANES), vm(RING, M, M * ROWS, LANES), *[vm(RING, M, ROWS, LANES)] * M,
-                pltpu.SMEM((4, L), F32), dma(8), dma(31), dma(8), *[dma(4)] * 6, pltpu.SemaphoreType.DMA],
+                pltpu.SMEM((4, L), F32), dma(8), pltpu.SemaphoreType.DMA, dma(31), dma(8), *[dma(4)] * 6, pltpu.SemaphoreType.DMA],
             compiler_params=pltpu.CompilerParams(collective_id=0, has_side_effects=True, vmem_limit_bytes=STEP_VMEM),
             name="ocean_step",
         )(vel_x, vel_y, pot_temp, salinity, stage)
@@ -648,8 +660,8 @@
             functools.partial(final_kernel, L),
             out_shape=[flat] * 3 + [cube] * 4,
             in_specs=[vmem_spec] * 11,
-            out_specs=[vmem_spec] * 3 + [hbm_spec] * 4,
-            scratch_shapes=[vm(4, M * len(STRIPS), L, SUB, 256), pltpu.SemaphoreType.DMA((4, M * len(STRIPS)))],
+            out_specs=[hbm_spec] * 7,
+            scratch_shapes=[vm(4, M * len(STRIPS), L, SUB, 256), pltpu.SemaphoreType.DMA((4, M * len(STRIPS))), dma(3)],
             name="ocean_final",
             compiler_params=pltpu.CompilerParams(vmem_limit_bytes=FINAL_VMEM),
         )(*sol, qu, qv, nuv, wet_levels, eta_o, tx_o, ty_o)

time: 42.4 us -> 40.9 us (0.965)
  local copies, waits for them, and re-layouts: 0.96 us -> 0.01 us
  Pallas kernels: 40.5 us -> 40 us
    unnamed x4 -> x2, local copies, waits for them, and re-layouts: 0.96 us -> 0.01 us
    pallas_call x1, Pallas kernels: 3.89 us -> 3.26 us  [local_step(): pl.pallas_call(functools.partial(final_kernel, L), out_shape=[flat] * 3 +...]
where the time goes in v8:
time: 40.9 us; the launch traced here: 40.7 us
  Pallas kernels  40 us (98%)
  between operations  0.67 us (2%)
    pallas_call x1, Pallas kernels, local_step(): pl.pallas_call(functools.partial(step_kernel, col_count, L, N), out_shape...  35.1 us
    pallas_call x1, Pallas kernels, local_step(): pl.pallas_call(functools.partial(final_kernel, L), out_shape=[flat] * 3 +...  3.26 us
    pallas_call x1, Pallas kernels, local_step(): pl.pallas_call(functools.partial(stage_kernel, N), out_shape=jax.ShapeDty...  1.7 us

profile of v8, /device:TPU:0, one launch (start us, length us, event | category | flops | bytes accessed | tf_op | source)
XLA Modules:
  0.0 40.7 jit_solution(9089438935556826287)
XLA Ops:
  0.6 1.7 %ocean_stage.1.stage_hbm = f32[2,240,2,24,128]{4,3,2,1,0:T(8,128)} custom-call(f32[2,24,256]{2,1,0:T(8,128)} %eta.1, f32[2,24,256]{2,1,0:T(8,128)} %tx.1, f32[2,24,256]{2,1,0:T(8,128)} %ty.1, f32[24,256]{1,0:T(8,128)} %depth.1, s32[24,256]{1,0:T(8,128)} %wet.1, f32[30]{0:T(128)} %weights.1), custom_call_target="tpu_custom_call" | custom-call | tf_op jit(solution)/shard_map/ocean_stage/pallas_call | solution.py:636
  2.3 0.0 copy-start
  2.4 35.1 %ocean_step.1 = (f32[36,2,2,24,128]{4,3,2,1,0:T(8,128)S(1)}, f32[36,2,2,24,128]{4,3,2,1,0:T(8,128)S(1)}, f32[36,2,2,24,128]{4,3,2,1,0:T(8,128)S(1)}, f32[36,2,2,...) custom-call(f32[36,2,24,256]{3,2,1,0:T(8,128)} %u_hbm.1, ...), custom_call_target="tpu_custom_call" | custom-call | tf_op jit(solution)/shard_map/ocean_step/pallas_call | solution.py:644
  37.4 0.0 copy-done
  37.4 3.3 %ocean_final.1 = (f32[2,24,256]{2,1,0:T(8,128)}, f32[2,24,256]{2,1,0:T(8,128)}, f32[2,24,256]{2,1,0:T(8,128)}, f32[36,2,24,256]{3,2,1,0:T(8,128)}, f32[36,2,24,2...) custom-call(f32[36,2,2,24,128]{4,3,2,1,0:T(8,128)S(1)} %get-tuple-element.17.sol_u, ...), custom_call_target="tpu_custom_call" | custom-call | tf_op jit(solution)/shard_map/ocean_final/pallas_call | solution.py:659
Async XLA Ops:
  2.3 35.1 %copy-start = (s32[24,256]{1,0:T(8,128)S(1)}, s32[24,256]{1,0:T(8,128)}, u32[]{:S(2)}) copy-start(s32[24,256]{1,0:T(8,128)} %wet.1) | copy-start | bytes 73732

commit v9 on v8

--- a/solution.py
+++ b/solution.py
@@ -22,7 +22,7 @@
 EDGE_BLOCK = 12
 TRACER_BLOCK = 36
 BACK_BLOCK = 36
-SUB_BLOCK = 3
+SUB_BLOCK = 5
 LEVEL_BLOCK = 36
 LANES = 128
 SUB = 8
@@ -70,13 +70,15 @@
 
 
 def east_block(x):
-    rolled = turn(x[:2], 127)
-    return jnp.where(lanes(2) == 127, jnp.concatenate([rolled[1:], x[2:]], axis=0), rolled)
+    rolled = turn(x[..., :2, :, :], 127)
+    following = jnp.concatenate([rolled[..., 1:, :, :], x[..., 2:, :, :]], axis=-3)
+    return jnp.where(iota(rolled.shape, x.ndim - 1) == 127, following, rolled)
 
 
 def west_block(x):
-    rolled = turn(x[:2], 1)
-    return jnp.where(lanes(2) == 0, jnp.concatenate([x[2:], rolled[:1]], axis=0), rolled)
+    rolled = turn(x[..., :2, :, :], 1)
+    before = jnp.concatenate([x[..., 2:, :, :], rolled[..., :1, :, :]], axis=-3)
+    return jnp.where(iota(rolled.shape, x.ndim - 1) == 0, before, rolled)
 
 
 STAGED = 6
@@ -472,19 +474,19 @@
     lax.fori_loop(0, M, back, 0)
 
     def tracer_init(m, rs):
-        return pair, lambda *a: None
-
-    def tracer(f):
-        def body(k, m, rs, get, e):
-            t, u = get(f, k, slice(0, 3)), get(U, k, slice(0, 3))
-            fx = u * (t + jnp.concatenate([east_block(t), t[:1]], axis=0))
-            t = t[OWN]
-            gain = fx[OWN] - west_block(fx) + (get(V, k, OWN) * (t + get(f, k, OWN, 1)) - get(V, k, OWN, -1) * (t + get(f, k, OWN, -1)))
-            e = (jnp.where(kmt[:, rs, :] > k.astype(F32), t - 0.5 * gain, 0.0) + DIFF_NUMBER * e) * table[3, k]
-            sol[f][k, m, :, rs, :] = e
-            return e
-
-        return body
+        return jnp.zeros((M, M, SUB, LANES), F32), lambda *a: None
+
+    def tracers(k, m, rs, get, e):
+        both = pl.ds(T, M)
+        t, u = get(both, k, slice(0, 3)), get(U, k, slice(0, 3))
+        fx = u * (t + jnp.concatenate([east_block(t), t[:, :1]], axis=1))
+        t = t[:, OWN]
+        gain = fx[:, OWN] - west_block(fx) + (
+            get(V, k, OWN) * (t + get(both, k, OWN, 1)) - get(V, k, OWN, -1) * (t + get(both, k, OWN, -1)))
+        e = (jnp.where(kmt[:, rs, :] > k.astype(F32), t - 0.5 * gain, 0.0) + DIFF_NUMBER * e) * table[3, k]
+        sol[T][k, m, :, rs, :] = e[0]
+        sol[S][k, m, :, rs, :] = e[1]
+        return e
 
     @pl.when(has_n)
     def _():
@@ -495,8 +497,7 @@
         to_n_later.wait_recv()
 
     lax.fori_loop(0, L // 4, unpack_rows_later, 0)
-    for f in (T, S):
-        for_strips(tracer(f), tracer_init, levels=TRACER_BLOCK)
+    for_strips(tracers, tracer_init, levels=TRACER_BLOCK)
     acc[...] = jnp.zeros(acc.shape, F32)
 
     collect(lambda m: fstage.at[m], lambda m: fstage_w.at[m], FX, 2, frow_sem, fe_sem, fw_sem, fpk_e, fpk_w)

time: 40.9 us -> 43.7 us (1.068)
  Pallas kernels: 40 us -> 42.9 us
    pallas_call x1, Pallas kernels: 35.1 us -> 37.9 us  [local_step(): pl.pallas_call(functools.partial(step_kernel, col_count, L, N), out_shape...]
where the time goes in v9:
time: 43.7 us; the launch traced here: 43.6 us
  Pallas kernels  42.9 us (98%)
  between operations  0.67 us (2%)
    pallas_call x1, Pallas kernels, local_step(): pl.pallas_call(functools.partial(step_kernel, col_count, L, N), out_shape...  37.9 us
    pallas_call x1, Pallas kernels, local_step(): pl.pallas_call(functools.partial(final_kernel, L), out_shape=[flat] * 3 +...  3.26 us
    pallas_call x1, Pallas kernels, local_step(): pl.pallas_call(functools.partial(stage_kernel, N), out_shape=jax.ShapeDty...  1.7 us

profile of v9, /device:TPU:0, one launch (start us, length us, event | category | flops | bytes accessed | tf_op | source)
XLA Modules:
  0.0 43.6 jit_solution(5265405448531179743)
XLA Ops:
  0.6 1.7 %ocean_stage.1.stage_hbm = f32[2,240,2,24,128]{4,3,2,1,0:T(8,128)} custom-call(f32[2,24,256]{2,1,0:T(8,128)} %eta.1, f32[2,24,256]{2,1,0:T(8,128)} %tx.1, f32[2,24,256]{2,1,0:T(8,128)} %ty.1, f32[24,256]{1,0:T(8,128)} %depth.1, s32[24,256]{1,0:T(8,128)} %wet.1, f32[30]{0:T(128)} %weights.1), custom_call_target="tpu_custom_call" | custom-call | tf_op jit(solution)/shard_map/ocean_stage/pallas_call | solution.py:637
  2.3 0.0 copy-start
  2.4 37.9 %ocean_step.1 = (f32[36,2,2,24,128]{4,3,2,1,0:T(8,128)S(1)}, f32[36,2,2,24,128]{4,3,2,1,0:T(8,128)S(1)}, f32[36,2,2,24,128]{4,3,2,1,0:T(8,128)S(1)}, f32[36,2,2,...) custom-call(f32[36,2,24,256]{3,2,1,0:T(8,128)} %u_hbm.1, ...), custom_call_target="tpu_custom_call" | custom-call | tf_op jit(solution)/shard_map/ocean_step/pallas_call | solution.py:645
  40.3 0.0 copy-done
  40.3 3.3 %ocean_final.1 = (f32[2,24,256]{2,1,0:T(8,128)}, f32[2,24,256]{2,1,0:T(8,128)}, f32[2,24,256]{2,1,0:T(8,128)}, f32[36,2,24,256]{3,2,1,0:T(8,128)}, f32[36,2,24,2...) custom-call(f32[36,2,2,24,128]{4,3,2,1,0:T(8,128)S(1)} %get-tuple-element.17.sol_u, ...), custom_call_target="tpu_custom_call" | custom-call | tf_op jit(solution)/shard_map/ocean_final/pallas_call | solution.py:660
Async XLA Ops:
  2.3 37.9 %copy-start = (s32[24,256]{1,0:T(8,128)S(1)}, s32[24,256]{1,0:T(8,128)}, u32[]{:S(2)}) copy-start(s32[24,256]{1,0:T(8,128)} %wet.1) | copy-start | bytes 73732

commit v10 on v8

--- a/solution.py
+++ b/solution.py
@@ -511,18 +511,18 @@
             div = (u - west(u)) + (v - frame[TY, :, pl.ds(base + SUB * t - 1, SUB), :])
             eta = frame[ETA, :, rs, :] - coef[0, :, rs, :] * div
             frame[ETA, :, rs, :] = eta
-            return u, v, eta
+            return eta
 
         last_row = iota((RING, SUB, LANES), 1) == SUB - 1
         following = eta_tile(0)
         for t in range(tiles):
-            u, v, e = following
+            e = following
             if t + 1 < tiles:
                 following = eta_tile(t + 1)
-            e_n = jnp.where(last_row, pltpu.roll(following[2], SUB - 1, 1), pltpu.roll(e, SUB - 1, 1))
+            e_n = jnp.where(last_row, pltpu.roll(following, SUB - 1, 1), pltpu.roll(e, SUB - 1, 1))
             rs = tile_rows(t)
-            frame[TX, :, rs, :] = u + frame[FX, :, rs, :] - coef[1, :, rs, :] * (east(e) - e)
-            frame[TY, :, rs, :] = v + frame[FY, :, rs, :] - coef[2, :, rs, :] * (e_n - e)
+            frame[TX, :, rs, :] += frame[FX, :, rs, :] - coef[1, :, rs, :] * (east(e) - e)
+            frame[TY, :, rs, :] += frame[FY, :, rs, :] - coef[2, :, rs, :] * (e_n - e)
         chip_rows = aligned(FPAD + (M * ROWS - SHIFT) * chip, M * ROWS)
         acc[...] += stage[1, KMT, n // ROWS, pl.ds(lax.rem(n, ROWS), 1), :] * frame[pl.ds(0, RING), OWN, chip_rows, :]
 

time: 40.9 us -> 40.9 us (level)
  no operation moved by 1% of the time
where the time goes in v10:
time: 40.9 us; the launch traced here: 40.7 us
  Pallas kernels  40.1 us (98%)
  between operations  0.67 us (2%)
    pallas_call x1, Pallas kernels, local_step(): pl.pallas_call(functools.partial(step_kernel, col_count, L, N), out_shape...  35.1 us
    pallas_call x1, Pallas kernels, local_step(): pl.pallas_call(functools.partial(final_kernel, L), out_shape=[flat] * 3 +...  3.26 us
    pallas_call x1, Pallas kernels, local_step(): pl.pallas_call(functools.partial(stage_kernel, N), out_shape=jax.ShapeDty...  1.7 us

profile of v10, /device:TPU:0, one launch (start us, length us, event | category | flops | bytes accessed | tf_op | source)
XLA Modules:
  0.0 40.7 jit_solution(10122010079643089996)
XLA Ops:
  0.6 1.7 %ocean_stage.1.stage_hbm = f32[2,240,2,24,128]{4,3,2,1,0:T(8,128)} custom-call(f32[2,24,256]{2,1,0:T(8,128)} %eta.1, f32[2,24,256]{2,1,0:T(8,128)} %tx.1, f32[2,24,256]{2,1,0:T(8,128)} %ty.1, f32[24,256]{1,0:T(8,128)} %depth.1, s32[24,256]{1,0:T(8,128)} %wet.1, f32[30]{0:T(128)} %weights.1), custom_call_target="tpu_custom_call" | custom-call | tf_op jit(solution)/shard_map/ocean_stage/pallas_call | solution.py:636
  2.3 0.0 copy-start
  2.4 35.1 %ocean_step.1 = (f32[36,2,2,24,128]{4,3,2,1,0:T(8,128)S(1)}, f32[36,2,2,24,128]{4,3,2,1,0:T(8,128)S(1)}, f32[36,2,2,24,128]{4,3,2,1,0:T(8,128)S(1)}, f32[36,2,2,...) custom-call(f32[36,2,24,256]{3,2,1,0:T(8,128)} %u_hbm.1, ...), custom_call_target="tpu_custom_call" | custom-call | tf_op jit(solution)/shard_map/ocean_step/pallas_call | solution.py:644
  37.5 0.0 copy-done
  37.5 3.3 %ocean_final.1 = (f32[2,24,256]{2,1,0:T(8,128)}, f32[2,24,256]{2,1,0:T(8,128)}, f32[2,24,256]{2,1,0:T(8,128)}, f32[36,2,24,256]{3,2,1,0:T(8,128)}, f32[36,2,24,2...) custom-call(f32[36,2,2,24,128]{4,3,2,1,0:T(8,128)S(1)} %get-tuple-element.17.sol_u, ...), custom_call_target="tpu_custom_call" | custom-call | tf_op jit(solution)/shard_map/ocean_final/pallas_call | solution.py:659
Async XLA Ops:
  2.3 35.1 %copy-start = (s32[24,256]{1,0:T(8,128)S(1)}, s32[24,256]{1,0:T(8,128)}, u32[]{:S(2)}) copy-start(s32[24,256]{1,0:T(8,128)} %wet.1) | copy-start | bytes 73732
